TPU v7x, 8 devices: a whole 2x2x1 slice. The times are simulated.
8 devices in a mesh: dp: 1 (over z), tp: 2 (over y), sp: 4 (over x, core).
Axes of the slice: x: 2, y: 2, z: 1, core: 2. Of those that a mesh axis runs over, the one named last changes fastest.
Arguments:
- hidden: bfloat16 [512, 4096], P('dp')
- ln_gain: bfloat16 [4096], replicated
- ln_bias: bfloat16 [4096], replicated
- w_q: bfloat16 [4096, 6144], P(None, 'tp')
- w_k: bfloat16 [4096, 1024], P(None, 'tp')
- w_v: bfloat16 [4096, 1024], P(None, 'tp')
- w_o: bfloat16 [6144, 4096], P('tp')
- k_cache: bfloat16 [512, 512, 8, 128], P('dp', 'sp', 'tp')
- v_cache: bfloat16 [512, 512, 8, 128], P('dp', 'sp', 'tp')
- lengths: int32 [512], P('dp')
Outputs:
- output 1: bfloat16 [512, 4096], P('dp')
- output 2: bfloat16 [512, 8, 128], P('dp', 'tp')
- output 3: bfloat16 [512, 8, 128], P('dp', 'tp')
All inputs are finite; a program needn't handle non-finite values.
Results may differ from a plain program's by a relative error of at most 0.00412719.
Values sent between devices are 32-bit elements.
A program may use at most 1 GiB of HBM per device.

v0:
```python
import jax
import jax.numpy as jnp
from jax import lax
from jax.sharding import PartitionSpec as P, NamedSharding


def norm_one_plus(hidden, ln_gain, ln_bias):
    wide = hidden.astype(jnp.float32)
    row_mean = jnp.mean(wide, axis=-1, keepdims=True)
    centred = wide - row_mean
    row_var = jnp.mean(centred * centred, axis=-1, keepdims=True)
    scaled = centred * lax.rsqrt(row_var + 1e-5)
    return (scaled * (1.0 + ln_gain.astype(jnp.float32)) + ln_bias.astype(jnp.float32)).astype(jnp.bfloat16)


def rotate_first(head_vecs, rot_pos, rot_dim):
    half_rot = rot_dim // 2
    inv_freq = 10000.0 ** (-2.0 * jnp.arange(half_rot, dtype=jnp.float32) / rot_dim)
    rot_angle = rot_pos.astype(jnp.float32)[..., None] * inv_freq
    cos_part = jnp.cos(rot_angle)
    sin_part = jnp.sin(rot_angle)
    lead_part = head_vecs[..., :half_rot]
    tail_part = head_vecs[..., half_rot:rot_dim]
    return jnp.concatenate([lead_part * cos_part - tail_part * sin_part, tail_part * cos_part + lead_part * sin_part, head_vecs[..., rot_dim:]], axis=-1)


def solution(mesh):
    def local_step(hidden, ln_gain, ln_bias, w_q, w_k, w_v, w_o, k_cache, v_cache, lengths):
        batch_rows, seq_local, kv_local, head_dim = k_cache.shape
        group_size = w_q.shape[1] // (head_dim * kv_local)
        rot_dim = head_dim // 2
        score_scale = head_dim ** -0.5
        normed = norm_one_plus(hidden, ln_gain, ln_bias)
        q_proj = jnp.dot(normed, w_q, preferred_element_type=jnp.float32).reshape(batch_rows, kv_local, group_size, head_dim)
        queries = rotate_first(q_proj, lengths[:, None, None], rot_dim).astype(jnp.bfloat16)
        k_proj = jnp.dot(normed, w_k, preferred_element_type=jnp.float32).reshape(batch_rows, kv_local, head_dim)
        k_new = rotate_first(k_proj, lengths[:, None], rot_dim).astype(jnp.bfloat16)
        v_new = jnp.dot(normed, w_v, preferred_element_type=jnp.float32).astype(jnp.bfloat16).reshape(batch_rows, kv_local, head_dim)
        block_index = lax.axis_index('sp')
        positions = block_index * seq_local + jnp.arange(seq_local)
        valid = positions[None, :] < lengths[:, None]
        scores = jnp.einsum('bkgd,bskd->bkgs', queries, k_cache, preferred_element_type=jnp.float32) * score_scale
        scores = jnp.where(valid[:, None, None, :], scores, -jnp.inf)
        owner = (lengths // seq_local) == block_index
        self_score = jnp.einsum('clhe,cle->clh', queries, k_new, preferred_element_type=jnp.float32) * score_scale
        self_score = jnp.where(owner[:, None, None], self_score, -jnp.inf)
        block_max = jnp.maximum(jnp.max(scores, axis=-1), self_score)
        safe_max = jnp.where(jnp.isfinite(block_max), block_max, 0.0)
        weights = jnp.exp(scores - safe_max[..., None])
        self_weight = jnp.exp(self_score - safe_max)
        weight_sum = jnp.sum(weights, axis=-1) + self_weight
        weighted = jnp.einsum('bkgs,bskd->bkgd', weights.astype(jnp.bfloat16), v_cache, preferred_element_type=jnp.float32)
        weighted = weighted + self_weight[..., None] * v_new.astype(jnp.float32)[:, :, None, :]
        packed = jnp.concatenate([weighted, block_max[..., None], weight_sum[..., None]], axis=-1)
        gathered = lax.all_gather(packed, 'sp', axis=0)
        all_max = gathered[..., head_dim]
        global_max = jnp.max(all_max, axis=0)
        factor = jnp.exp(all_max - global_max)
        total = jnp.sum(gathered[..., head_dim + 1] * factor, axis=0)
        context = jnp.sum(gathered[..., :head_dim] * factor[..., None], axis=0) / total[..., None]
        context = context.astype(jnp.bfloat16).reshape(batch_rows, kv_local * group_size * head_dim)
        partial_out = jnp.dot(context, w_o, preferred_element_type=jnp.float32)
        summed = lax.psum(partial_out, 'tp')
        out = (hidden.astype(jnp.float32) + summed).astype(jnp.bfloat16)
        return out, k_new, v_new

    row_spec = P('dp', None)
    cache_spec = P('dp', 'sp', 'tp', None)
    head_spec = P('dp', 'tp', None)
    return jax.shard_map(local_step, mesh=mesh, in_specs=(row_spec, P(None), P(None), P(None, 'tp'), P(None, 'tp'), P(None, 'tp'), P('tp', None), cache_spec, cache_spec, P('dp')), out_specs=(row_spec, head_spec, head_spec), check_vma=False)
```

profile of v0, /device:TPU:0, one launch (start us, length us, event | category | flops | bytes accessed | tf_op | source)
XLA Modules:
  0.0 662.8 jit_solution(15610868735430760925)
XLA Ops:
  17.6 18.9 %fusion.42 = f32[512,3072]{0,1:T(8,128)} fusion(bf16[512,4096]{1,0:T(8,128)(2,1)S(1)} %fusion.10, bf16[4096,3072]{1,0:T(8,128)(2,1)} %param.13), kind=kOutput, calls=%fused_computation.72 | convolution fusion | flops 12884901888 | bytes 35651584 | tf_op jit(solution)/shard_map/dot_general | solution.py:34
  38.6 3.5 fusion.40
  42.3 6.6 %convolution_convert_fusion = bf16[512,512]{0,1:T(8,128)(2,1)} fusion(bf16[512,4096]{1,0:T(8,128)(2,1)} %copy-done.10, bf16[4096,512]{1,0:T(8,128)(2,1)} %param.15), kind=kOutput, calls=%fused_computation.35 | convolution fusion | flops 2147745792 | bytes 8912896 | tf_op jit(solution)/shard_map/dot_general | solution.py:38
  61.8 5.1 copy.152
  66.8 4.0 copy.151
  73.7 6.0 subtract_convert_fusion
  80.9 3.1 pad_maximum_fusion.1
  84.0 3.6 fusion.15
  87.7 42.9 %fusion.12 = (f32[512,4,6]{2,1,0:T(4,128)}, f32[512,4,6,128]{3,2,1,0:T(8,128)}) fusion(pred[512,128]{1,0:T(8,128)(4,1)S(1)} %broadcast_compare_fusion, bf16[512,128,4,128]{3,2,1,0:T(4,128)(2,1)} %param.17, bf16[512,4,6,128]{3,0,2,1:T(8,128)(2,1)S(1)} %pad_maximum_fusion.1), kind=kOutput, calls=%fused_computation.20 | convolution fusion | flops 407359488 | bytes 76660736 | tf_op jit(solution)/shard_map/bkgd,bskd->bkgs/dot_general | solution.py:42
  130.6 3.4 is-finite_select_fusion
  134.3 13.2 %fusion.13 = f32[512,4,6]{2,1,0:T(4,128)S(1)} fusion(f32[512,4,6,128]{3,2,1,0:T(8,128)} %get-tuple-element.42, f32[512,4,6]{2,1,0:T(4,128)S(1)} %get-tuple-element.26, pred[512,128]{1,0:T(8,128)(4,1)S(1)} %broadcast_compare_fusion), kind=kLoop, calls=%fused_computation.21 | loop fusion | flops 6279168 | bytes 6455296 | tf_op jit(solution)/shard_map/reduce_sum | solution.py:51
  147.5 3.2 fusion.37
  150.7 32.4 %multiply_add_fusion = f32[512,4,6,128]{3,2,1,0:T(8,128)} fusion(f32[512,4,128]{2,1,0:T(4,128)} %copy.127, f32[512,4,6]{2,1,0:T(4,128)} %get-tuple-element.25, bf16[512,128,4,128]{3,2,1,0:T(4,128)(2,1)} %param.18, f32[512,4,6,128]{3,2,1,0:T(8,128)} %get-tuple-element.42, f32[512,4,6]{2,1,0:T(4,128)S(1)} %get-tuple-element.26, ...), kind=kOutput, calls=%fused_computation.17 | convolution fusion | flops 412090368 | bytes 80904192 | tf_op jit(solution)/shard_map/bkgs,bskd->bkgd/dot_general | solution.py:52
  183.1 8.2 %copy.130 = f32[512,4,6,128]{0,1,3,2:T(4,128)} copy(f32[512,4,6,128]{3,2,1,0:T(8,128)} %multiply_add_fusion) | data formatting | bytes 12582912 | tf_op jit(solution)/shard_map/add | solution.py:53
  191.6 7.1 %pad_maximum_fusion = f32[512,4,6,130]{0,1,3,2:T(4,128)} fusion(f32[512,4,6,1]{0,1,3,2:T(4,128)S(1)} %bitcast.44, f32[512,4,6,1]{0,1,3,2:T(4,128)S(1)} %bitcast.43, f32[512,4,6,128]{0,1,3,2:T(4,128)} %copy.130), kind=kLoop, calls=%fused_computation.23 | loop fusion | flops 3194880 | bytes 12779520 | tf_op jit(solution)/shard_map/concatenate | solution.py:54
  198.8 158.0 %all-gather.3.cloned.1.call-done = f32[2048,4,6,130]{0,1,3,2:T(4,128)} async-done(((f32[512,4,6,130]{0,1,3,2:T(4,128)}), f32[2048,4,6,130]{0,1,3,2:T(4,128)}) %all-gather.3.cloned.1.call-update) | async-done | bytes 25559056 | tf_op jit(solution)/shard_map/all_gather | solution.py:55
  356.7 33.2 %reshape.199 = f32[4,512,4,6,130]{1,0,2,4,3:T(4,128)} reshape(f32[2048,4,6,130]{0,1,3,2:T(4,128)} %all-gather.3.cloned.1.call-done) | data formatting | bytes 51118080 | tf_op jit(solution)/shard_map/all_gather | solution.py:55
  391.5 20.9 %fusion.4 = f32[512,4,6,128]{0,3,2,1:T(8,128)} fusion(f32[4,512,4,6]{1,0,3,2:T(4,128)S(1)} %exponential_bitcast_fusion, f32[4,512,4,6,130]{1,0,2,4,3:T(4,128)} %reshape.199), kind=kLoop, calls=%fused_computation.5 | loop fusion | flops 11010048 | bytes 31653888 | tf_op jit(solution)/shard_map/reduce_sum | solution.py:60
  412.8 9.5 %copy.144 = f32[512,4,6,128]{3,2,1,0:T(8,128)} copy(f32[512,4,6,128]{0,3,2,1:T(8,128)} %fusion.4) | data formatting | bytes 12582912
  422.3 6.8 %divide_convert_fusion = bf16[512,4,6,128]{3,2,1,0:T(8,128)(2,1)} fusion(f32[512,4,6,128]{3,2,1,0:T(8,128)} %copy.144, f32[512,4,6]{2,1,0:T(4,128)S(1)} %copy.136), kind=kLoop, calls=%fused_computation.16 | loop fusion | flops 3145728 | bytes 9486336 | tf_op jit(solution)/shard_map/convert_element_type | solution.py:61
  429.1 5.5 copy.137
  434.6 20.4 %fusion.44 = f32[512,4096]{1,0:T(8,128)} fusion(bf16[512,3072]{0,1:T(8,128)(2,1)S(1)} %bitcast.38, bf16[3072,4096]{1,0:T(8,128)(2,1)} %param.16), kind=kOutput, calls=%fused_computation.74 | convolution fusion | flops 12884901888 | bytes 36700160 | tf_op jit(solution)/shard_map/dot_general | solution.py:62
  459.1 188.3 %all-reduce.2.cloned.1.call-done = f32[512,4096]{1,0:T(8,128)} async-done(((f32[512,4096]{1,0:T(8,128)}), f32[512,4096]{1,0:T(8,128)}) %all-reduce.2.cloned.1.call-update) | async-done | bytes 8388624 | tf_op jit(solution)/shard_map/psum | solution.py:63
  647.5 8.0 %fusion.11 = bf16[512,4096]{1,0:T(8,128)(2,1)} fusion(f32[512,4096]{1,0:T(8,128)} %all-reduce.2.cloned.1.call-done, bf16[512,4096]{1,0:T(8,128)(2,1)} %param.10), kind=kLoop, calls=%fused_computation.15 | loop fusion | flops 6291456 | bytes 16777216 | tf_op jit(solution)/shard_map/convert_element_type | solution.py:64
  (72 shorter events, 36.1 us)
Async XLA Ops:
  7.2 4.7 copy-start.14
  7.2 349.6 %all-gather.3.cloned.1.call-start = ((), (), s32[]{:S(2)}) async-start(), calls=%async_computation.1 | async-start | bytes 31948800 | tf_op jit(solution)/shard_map/all_gather | solution.py:55
  7.2 3.5 copy-start
  7.2 4.7 copy-start.15
  10.2 4.0 copy-start.16
  14.2 3.3 copy-start.10
  36.5 5.6 copy-start.13
  61.8 10.1 %copy-start.8 = (f32[512,4,32]{2,1,0:T(4,128)S(1)}, f32[512,4,32]{2,1,0:T(4,128)}, u32[]{:S(2)}) copy-start(f32[512,4,32]{2,1,0:T(4,128)} %copy.155) | copy-start | bytes 786436
  73.7 6.0 copy-start.2
  73.7 6.0 copy-start.4
  73.7 6.0 copy-start.6
  73.7 7.2 %copy-start.1 = (bf16[512,4,6,64]{3,0,2,1:T(8,128)(2,1)S(1)}, bf16[512,4,6,64]{3,0,2,1:T(8,128)(2,1)}, u32[]{:S(2)}) copy-start(bf16[512,4,6,64]{3,0,2,1:T(8,128)(2,1)} %copy.153) | copy-start | bytes 4718596
  134.0 13.5 %copy-start.9 = (f32[512,4,1,6]{3,2,1,0:T(1,128)S(1)}, f32[512,4,1,6]{3,2,1,0:T(1,128)}, u32[]{:S(2)}) copy-start(f32[512,4,1,6]{3,2,1,0:T(1,128)} %fusion.15) | copy-start | bytes 147460
  183.1 8.2 %copy-start.11 = (f32[512,4,6]{2,1,0:T(4,128)S(1)}, f32[512,4,6]{2,1,0:T(4,128)}, u32[]{:S(2)}) copy-start(f32[512,4,6]{2,1,0:T(4,128)} %get-tuple-element.24) | copy-start | bytes 147460
  198.7 448.8 %all-reduce.2.cloned.1.call-start = ((), (), s32[]{:S(2)}) async-start(), calls=%async_computation | async-start | bytes 16777216 | tf_op jit(solution)/shard_map/psum | solution.py:63
  455.1 1.0 copy-start.12
  455.1 2.1 copy-start.3
  455.1 2.1 copy-start.5
  455.1 2.1 copy-start.7
Sparse Core Ops, SparseCore 0:
  198.8 157.8 all-gather.2
  455.3 192.1 all-reduce.1
where the time goes:
time: 672 us; the launch traced here: 663 us
  waiting for transfers between devices  346 us (51%)
  matrix products  127 us (19%)
  local copies, waits for them, and re-layouts  88.5 us (13%)
  other arithmetic  85.6 us (13%)
  between operations  14.9 us (2%)
    psum x1, waiting for transfers between devices, local_step(): summed = lax.psum(partial_out, 'tp')  188 us
    all_gather x1, waiting for transfers between devices, local_step(): gathered = lax.all_gather(packed, 'sp', axis=0)  158 us
    dot_general x1, matrix products, local_step(): jnp.einsum('bkgd,bskd->bkgs', queries, k_cache, preferred_element_type=jn...  42.9 us
    all_gather x1, local copies, waits for them, and re-layouts, local_step(): gathered = lax.all_gather(packed, 'sp', axis=0)  33.2 us
    dot_general x1, matrix products, local_step(): jnp.einsum('bkgs,bskd->bkgd', weights.astype(jnp.bfloat16), v_cache, pref...  32.4 us
    unnamed x43, local copies, waits for them, and re-layouts  29.5 us
    reduce_sum x1, other arithmetic, local_step(): jnp.sum(gathered[..., :head_dim] * factor[..., None], axis=0)  20.9 us
    dot_general x1, matrix products, local_step(): partial_out = jnp.dot(context, w_o, preferred_element_type=jnp.float32)  20.4 us
  transfers between devices with their start and end apart: 2, of which 2 were waited for; matrix products, arithmetic and copies ran while one was open for 0% of the time, Pallas kernels for 0%

commit v1 on v0

v1 whole, which is shorter than its diff:
```python
import functools
import jax
import jax.numpy as jnp
from jax import lax
from jax.experimental import pallas as pl
from jax.experimental.pallas import tpu as pltpu
from jax.sharding import PartitionSpec as P

MESH = pl.DeviceIdType.MESH
D = 128
G = 24
KV = 4
ROWS = 512
DM = 4096
OWN = 128
STEP = 4
NSTEP = OWN // STEP
NCH = 4
CR = OWN // NCH
SPC = NSTEP // NCH
HALF = DM // 2
NEG = -3e38
FLOOR = -1e38
SCALE2 = (128 ** -0.5) * 1.4426950408889634
F32 = jnp.float32
BF16 = jnp.bfloat16

(KD, KDS, KX, KXS, KY, KFX, KFY, KFC, KGY, KGCX, KGCY, KGCD) = range(12)


def qkv_kernel(h_ref, g_ref, b_ref, cos_ref, s1_ref, s2_ref, wq_ref, wk_ref, wv_ref,
               q_ref, k_ref, v_ref, hn, wbuf, res, kvf, sems):
    i = pl.program_id(0)
    nq = 6

    def fetch(t, slot):
        @pl.when(t < nq)
        def _():
            pltpu.make_async_copy(wq_ref.at[:, pl.ds(pl.multiple_of(t * 512, 512), 512)], wbuf.at[slot], sems.at[slot]).start()

        @pl.when(t == nq)
        def _():
            pltpu.make_async_copy(wk_ref, wbuf.at[slot], sems.at[slot]).start()

        @pl.when(t == nq + 1)
        def _():
            pltpu.make_async_copy(wv_ref, wbuf.at[slot], sems.at[slot]).start()

    @pl.when(i == 0)
    def _():
        fetch(i, 0)
        gain = 1.0 + g_ref[...].astype(F32)
        bias = b_ref[...].astype(F32)

        def norm(r, _):
            rows = pl.ds(pl.multiple_of(r * 16, 16), 16)
            wide = h_ref[rows, :].astype(F32)
            mean = jnp.mean(wide, axis=1, keepdims=True)
            cen = wide - mean
            var = jnp.mean(cen * cen, axis=1, keepdims=True)
            hn[rows, :] = ((cen * lax.rsqrt(var + 1e-5)) * gain + bias).astype(BF16)
            return 0
        lax.fori_loop(0, ROWS // 16, norm, 0)

    slot = lax.rem(i, 2)

    @pl.when(i < nq + 1)
    def _():
        fetch(i + 1, 1 - slot)
    pltpu.make_async_copy(wk_ref, wbuf.at[slot], sems.at[slot]).wait()
    res[...] = jnp.dot(hn[...], wbuf[slot], preferred_element_type=F32)

    def rope(x, rows):
        return x * cos_ref[rows, :] + pltpu.roll(x, 96, 1) * s1_ref[rows, :] + pltpu.roll(x, 32, 1) * s2_ref[rows, :]

    @pl.when(i < nq)
    def _():
        def body(r, _):
            rows = pl.ds(pl.multiple_of(r * 64, 64), 64)
            for u in range(4):
                x = rope(res[rows, u * D:(u + 1) * D], rows)
                q_ref[pl.ds(r * (64 * G) + i * 4 + u, 64, G), :] = x
            return 0
        lax.fori_loop(0, ROWS // 64, body, 0)

    @pl.when(i == nq)
    def _():
        def body(r, _):
            rows = pl.ds(pl.multiple_of(r * 64, 64), 64)
            for u in range(KV):
                kvf[pl.ds(r * (64 * KV) + u, 64, KV), :] = rope(res[rows, u * D:(u + 1) * D], rows)
            return 0
        lax.fori_loop(0, ROWS // 64, body, 0)
        k_ref[...] = kvf[...].astype(BF16)

    @pl.when(i == nq + 1)
    def _():
        def body(r, _):
            rows = pl.ds(pl.multiple_of(r * 64, 64), 64)
            for u in range(KV):
                kvf[pl.ds(r * (64 * KV) + u, 64, KV), :] = res[rows, u * D:(u + 1) * D]
            return 0
        lax.fori_loop(0, ROWS // 64, body, 0)
        v_ref[...] = kvf[...].astype(BF16)


def project(hidden, ln_gain, ln_bias, cos_t, s1_t, s2_t, w_q, w_k, w_v):
    vm = pl.BlockSpec(memory_space=pltpu.VMEM)
    hbm = pl.BlockSpec(memory_space=pl.ANY)
    return pl.pallas_call(
        qkv_kernel,
        grid=(8,),
        out_shape=(jax.ShapeDtypeStruct((ROWS * G, D), F32),
                   jax.ShapeDtypeStruct((ROWS * KV, D), BF16),
                   jax.ShapeDtypeStruct((ROWS * KV, D), BF16)),
        in_specs=[vm] * 6 + [hbm] * 3,
        out_specs=(vm, vm, vm),
        scratch_shapes=[pltpu.VMEM((ROWS, DM), BF16), pltpu.VMEM((2, DM, 512), BF16), pltpu.VMEM((ROWS, 512), F32),
                        pltpu.VMEM((ROWS * KV, D), F32), pltpu.SemaphoreType.DMA((2,))],
        compiler_params=pltpu.CompilerParams(vmem_limit_bytes=48 * 1024 * 1024, dimension_semantics=("arbitrary",)),
        cost_estimate=pl.CostEstimate(flops=2 * ROWS * DM * 4096, bytes_accessed=48 << 20, transcendentals=0),
        name="qkv",
    )(hidden, ln_gain, ln_bias, cos_t, s1_t, s2_t, w_q, w_k, w_v)


def attn_kernel(events, lens_ref, q_ref, k_ref, v_ref, qh_ref, kn_ref, vn_ref, hid_ref, wo_ref, out_ref,
                pos, acc, st, drecv, dst, cst, xrecv, xst, pout, yrecv, obuf, wo, qown, knb, vnb, knf, vnf, hid,
                ctxf, lhs, stage, lsem, osem, ssem, rsem):
    i = pl.program_id(0)
    dp = lax.axis_index("dp")
    y = lax.axis_index("tp")
    s = lax.axis_index("sp")
    x = s // 2
    c = lax.rem(s, 2)
    nx, nc, ny = 1 - x, 1 - c, 1 - y
    dev_c = (dp, y, 2 * x + nc)
    dev_x = (dp, y, 2 * nx + c)
    dev_y = (dp, ny, s)
    own = 2 * x + c
    own_x = 2 * nx + c
    base = s * 128

    def remote(kind, ch, src, dst_, dev):
        return pltpu.make_async_remote_copy(src_ref=src, dst_ref=dst_, send_sem=ssem.at[kind, ch], recv_sem=rsem.at[kind, ch],
                                            device_id=dev, device_id_type=MESH)

    locals_ = [
        (wo_ref, wo), (qh_ref.at[x, c], qown), (kn_ref.at[x, c], knb), (vn_ref.at[x, c], vnb), (hid_ref.at[x, c], hid),
    ]

    def local_copy(n):
        a, b = locals_[n]
        return pltpu.make_async_copy(a, b, lsem.at[n])

    @pl.when(i == 0)
    def _():
        sem = pltpu.get_barrier_semaphore()
        for dev in (dev_c, dev_x, dev_y):
            pl.semaphore_signal(sem, inc=1, device_id=dev, device_id_type=MESH)
        for n in range(len(locals_)):
            local_copy(n).start()
        col = lax.broadcasted_iota(jnp.int32, (48, 512), 1)
        row = lax.broadcasted_iota(jnp.int32, (48, 512), 0)
        jj = jnp.where(row >= G, row - G, row)
        head = (jj >= 6).astype(jnp.int32) + (jj >= 12).astype(jnp.int32) + (jj >= 18).astype(jnp.int32)
        pos[...] = jnp.where((col & 3) == head, col >> 2, 1 << 20)
        pl.semaphore_wait(sem, 3)

    lane = lax.broadcasted_iota(jnp.int32, (48, D), 1)
    low = lax.broadcasted_iota(jnp.int32, (48, D), 0) < G
    low1 = lax.broadcasted_iota(jnp.int32, (48, 1), 0) < G

    @pl.when(i < NSTEP)
    def _():
        ch = i // SPC
        within = lax.rem(i, SPC)
        for xo in range(2):
            for co in range(2):
                stats = jnp.where(within == 0, 0.0, st[ch, co, xo])
                for pp in range(STEP // 2):
                    q48 = q_ref[xo, co, pp * 48:(pp + 1) * 48, :]
                    qbd = jnp.concatenate([jnp.where(low, q48, 0.0), jnp.where(low, 0.0, q48)], axis=1).astype(BF16)
                    kk = jnp.concatenate([k_ref[xo, co, 2 * pp], k_ref[xo, co, 2 * pp + 1]], axis=1)
                    sc = lax.dot_general(qbd, kk, (((1,), (1,)), ((), ())), preferred_element_type=F32)
                    r0 = (2 * xo + co) * OWN + i * STEP + 2 * pp
                    lenv = jnp.where(low1, lens_ref[r0] - base, lens_ref[r0 + 1] - base)
                    sc = jnp.where(pos[...] < lenv, sc * SCALE2, NEG)
                    m = jnp.maximum(jnp.max(sc, axis=1, keepdims=True), FLOOR)
                    w = jnp.exp2(sc - m)
                    l = jnp.sum(w, axis=1, keepdims=True)
                    vv = jnp.concatenate([v_ref[xo, co, 2 * pp], v_ref[xo, co, 2 * pp + 1]], axis=1)
                    o = jnp.dot(w.astype(BF16), vv, preferred_element_type=F32)
                    at = pl.multiple_of((i * STEP + 2 * pp) * G, 2 * G)
                    acc[co, xo, pl.ds(at, G), :] = o[:G, :D]
                    acc[co, xo, pl.ds(at + G, G), :] = o[G:, D:]
                    idx = within * (STEP // 2) + pp
                    stats = jnp.where(lane == idx, m, jnp.where(lane == idx + 64, l, stats))
                st[ch, co, xo] = stats

    def pick(block, n):
        m = jnp.sum(jnp.where(lane == n, block, 0.0), axis=1, keepdims=True)
        l = jnp.sum(jnp.where(lane == n + 64, block, 0.0), axis=1, keepdims=True)
        return m, l

    def crows(ch):
        return pl.ds(ch * CR * G, CR * G)

    def c_acc(ch):
        return remote(KD, ch, acc.at[nc, :, crows(ch)], drecv.at[:, crows(ch)], dev_c)

    def c_st(ch):
        return remote(KDS, ch, st.at[ch, nc], dst.at[ch], dev_c)

    def x_acc(ch):
        return remote(KX, ch, acc.at[c, nx, crows(ch)], xrecv.at[crows(ch)], dev_x)

    def x_st(ch):
        return remote(KXS, ch, cst.at[ch, nx], xst.at[ch], dev_x)

    def y_part(ch):
        return remote(KY, ch, pout.at[ch, ny], yrecv.at[ch], dev_y)

    def piece(half, owner, ch):
        return obuf.at[half, owner, pl.ds(ch * CR, CR)]

    def gather(kind, ch, dev, half, owner):
        return remote(kind, ch, piece(half, owner, ch), piece(half, owner, ch), dev)

    own_c = 2 * x + nc
    own_xc = 2 * nx + nc

    def ev_core(ch):
        c_acc(ch).start()
        c_st(ch).start()

    def ev_x(ch):
        c_acc(ch).wait_recv()
        c_st(ch).wait_recv()

        def merge(xo, order):
            mine = st[ch, c, xo]
            theirs = dst[ch, xo]

            def body(n, out):
                rows = pl.ds(pl.multiple_of((ch * CR + 2 * n) * G, 2 * G), 2 * G)
                ma, la = pick(mine, n)
                mb, lb = pick(theirs, n)
                m = jnp.maximum(ma, mb)
                fa, fb = jnp.exp2(ma - m), jnp.exp2(mb - m)
                acc[c, xo, rows, :] = acc[c, xo, rows, :] * fa + drecv[xo, rows, :] * fb
                return jnp.where(lane == n, m, jnp.where(lane == n + 64, la * fa + lb * fb, out))
            cst[ch, xo] = lax.fori_loop(0, CR // 2, body, jnp.zeros((48, D), F32))
        merge(nx, 0)
        x_acc(ch).start()
        x_st(ch).start()
        merge(x, 1)

    def ev_proj(ch):
        if ch == 0:
            for n in range(len(locals_)):
                local_copy(n).wait()
            knf[...] = knb[...].astype(F32)
            vnf[...] = vnb[...].astype(F32)
        x_acc(ch).wait_recv()
        x_st(ch).wait_recv()
        mine = cst[ch, x]
        theirs = xst[ch]
        rr = lax.broadcasted_iota(jnp.int32, (48, 8), 0)
        cc = lax.broadcasted_iota(jnp.int32, (48, 8), 1)
        spread = ((rr >= cc * 6) & (rr < cc * 6 + 6)).astype(F32)

        def body(n, _):
            rows = pl.ds(pl.multiple_of((ch * CR + 2 * n) * G, 2 * G), 2 * G)
            krows = pl.ds(pl.multiple_of((ch * CR + 2 * n) * KV, 2 * KV), 2 * KV)
            kx = jnp.dot(spread, knf[krows, :], preferred_element_type=F32)
            vx = jnp.dot(spread, vnf[krows, :], preferred_element_type=F32)
            ms = jnp.sum(qown[rows, :].astype(BF16).astype(F32) * kx, axis=1, keepdims=True) * SCALE2
            ma, la = pick(mine, n)
            mb, lb = pick(theirs, n)
            m = jnp.maximum(jnp.maximum(ma, mb), ms)
            fa, fb, fs = jnp.exp2(ma - m), jnp.exp2(mb - m), jnp.exp2(ms - m)
            tot = la * fa + lb * fb + fs
            ctx = acc[c, x, rows, :] * fa + xrecv[rows, :] * fb + fs * vx
            ctxf[pl.ds(pl.multiple_of(n * 48, 48), 48), :] = ctx / tot
            return 0
        lax.fori_loop(0, CR // 2, body, 0)
        for j in range(G):
            lhs[:, j * D:(j + 1) * D] = ctxf[pl.ds(j, CR, G), :].astype(BF16)

        for half in range(2):
            def mm(n, _, half=half):
                cols = pl.ds(pl.multiple_of(half * HALF + n * 512, 512), 512)
                pout[ch, half, :, pl.ds(pl.multiple_of(n * 512, 512), 512)] = jnp.dot(lhs[...], wo[:, cols], preferred_element_type=F32)
                return 0
            lax.fori_loop(0, HALF // 512, mm, 0)
        y_part(ch).start()

    def ev_sum(ch):
        y_part(ch).wait_recv()
        rows = pl.ds(ch * CR, CR)

        def body(n, _):
            cols = pl.ds(pl.multiple_of(n * 512, 512), 512)
            hcols = pl.ds(pl.multiple_of(y * HALF + n * 512, 512), 512)
            obuf[y, own, rows, cols] = pout[ch, y, :, cols] + yrecv[ch, :, cols] + hid[rows, hcols].astype(F32)
            return 0
        lax.fori_loop(0, HALF // 512, body, 0)
        gather(KFX, ch, dev_x, y, own).start()
        gather(KFY, ch, dev_y, y, own).start()
        gather(KFC, ch, dev_c, y, own).start()

    def ev_fwd(ch):
        gather(KFX, ch, dev_x, y, own_x).wait_recv()
        gather(KGY, ch, dev_y, y, own_x).start()
        gather(KGCX, ch, dev_c, y, own_x).start()
        gather(KFY, ch, dev_y, ny, own).wait_recv()
        gather(KGCY, ch, dev_c, ny, own).start()

    def ev_last(ch):
        gather(KGY, ch, dev_y, ny, own_x).wait_recv()
        gather(KGCD, ch, dev_c, ny, own_x).start()

    def out_copy(ch):
        return pltpu.make_async_copy(stage.at[ch % 2], out_ref.at[:, pl.ds(ch * CR, CR)], osem.at[ch % 2])

    def ev_out(ch):
        gather(KFC, ch, dev_c, y, own_c).wait_recv()
        gather(KGCX, ch, dev_c, y, own_xc).wait_recv()
        gather(KGCY, ch, dev_c, ny, own_c).wait_recv()
        gather(KGCD, ch, dev_c, ny, own_xc).wait_recv()
        if ch >= 2:
            out_copy(ch - 2).wait()
        rows = pl.ds(ch * CR, CR)

        def body(n, _):
            for half in range(2):
                for q4 in range(4):
                    stage[ch % 2, n, :, half * HALF + q4 * 512:half * HALF + (q4 + 1) * 512] = obuf[half, n, rows, q4 * 512:(q4 + 1) * 512].astype(BF16)
            return 0
        lax.fori_loop(0, 4, body, 0)
        out_copy(ch).start()

    def ev_drain(ch):
        c_acc(ch).wait_send()
        c_st(ch).wait_send()
        x_acc(ch).wait_send()
        x_st(ch).wait_send()
        y_part(ch).wait_send()
        for kind, dev, half, owner in ((KFX, dev_x, y, own), (KFY, dev_y, y, own), (KFC, dev_c, y, own), (KGY, dev_y, y, own_x),
                                       (KGCX, dev_c, y, own_x), (KGCY, dev_c, ny, own), (KGCD, dev_c, ny, own_x)):
            gather(kind, ch, dev, half, owner).wait_send()
        if ch >= NCH - 2:
            out_copy(ch).wait()

    table = {"core": ev_core, "x": ev_x, "proj": ev_proj, "sum": ev_sum, "fwd": ev_fwd, "last": ev_last, "out": ev_out, "drain": ev_drain}
    for when, names in events:
        @pl.when(i == when)
        def _(names=names):
            for name, ch in names:
                table[name](ch)


def schedule():
    offs = (("core", 0), ("x", 2), ("proj", 10), ("sum", 16), ("fwd", 20), ("last", 23), ("out", 25))
    order = {name: n for n, (name, _) in enumerate(offs)}
    plan = {}
    for ch in range(NCH):
        first = SPC * (ch + 1) - 1
        for name, off in offs:
            plan.setdefault(min(first + off, NSTEP - 1 + 64), []).append((first + off, order[name], name, ch))
    steps = {}
    for at in sorted(plan):
        for t, o, name, ch in sorted(plan[at]):
            steps.setdefault(min(at, NSTEP), []).append((t, o, name, ch))
    out = []
    for at in sorted(steps):
        out.append((at, tuple((name, ch) for _, _, name, ch in sorted(steps[at]))))
    last = out[-1]
    out[-1] = (last[0], last[1] + tuple(("drain", ch) for ch in range(NCH)))
    return tuple(out)


def attend(lengths, q, k_cache, v_cache, kn, vn, hidden, w_o):
    hbm = pl.BlockSpec(memory_space=pl.ANY)
    hold = NSTEP - 1
    cache_spec = pl.BlockSpec((2, 2, STEP, 512, D), lambda i: (0, 0, jnp.minimum(i, hold), 0, 0))
    return pl.pallas_call(
        functools.partial(attn_kernel, schedule()),
        grid=(NSTEP + 1,),
        out_shape=jax.ShapeDtypeStruct((4, OWN, DM), BF16),
        in_specs=[pl.BlockSpec(memory_space=pltpu.SMEM),
                  pl.BlockSpec((2, 2, STEP * G, D), lambda i: (0, 0, jnp.minimum(i, hold), 0)),
                  cache_spec, cache_spec, hbm, hbm, hbm, hbm, hbm],
        out_specs=hbm,
        scratch_shapes=[
            pltpu.VMEM((48, 512), jnp.int32),
            pltpu.VMEM((2, 2, OWN * G, D), F32),
            pltpu.VMEM((NCH, 2, 2, 48, D), F32),
            pltpu.VMEM((2, OWN * G, D), F32),
            pltpu.VMEM((NCH, 2, 48, D), F32),
            pltpu.VMEM((NCH, 2, 48, D), F32),
            pltpu.VMEM((OWN * G, D), F32),
            pltpu.VMEM((NCH, 48, D), F32),
            pltpu.VMEM((NCH, 2, CR, HALF), F32),
            pltpu.VMEM((NCH, CR, HALF), F32),
            pltpu.VMEM((2, 4, OWN, HALF), F32),
            pltpu.VMEM((G * D, DM), BF16),
            pltpu.VMEM((OWN * G, D), F32),
            pltpu.VMEM((OWN * KV, D), BF16),
            pltpu.VMEM((OWN * KV, D), BF16),
            pltpu.VMEM((OWN * KV, D), F32),
            pltpu.VMEM((OWN * KV, D), F32),
            pltpu.VMEM((OWN, DM), BF16),
            pltpu.VMEM((CR * G, D), F32),
            pltpu.VMEM((CR, G * D), BF16),
            pltpu.VMEM((2, 4, CR, DM), BF16),
            pltpu.SemaphoreType.DMA((5,)),
            pltpu.SemaphoreType.DMA((2,)),
            pltpu.SemaphoreType.DMA((12, NCH)),
            pltpu.SemaphoreType.DMA((12, NCH)),
        ],
        compiler_params=pltpu.CompilerParams(vmem_limit_bytes=67043328, collective_id=0, has_side_effects=True,
                                             dimension_semantics=("arbitrary",)),
        cost_estimate=pl.CostEstimate(flops=10 ** 10, bytes_accessed=170 << 20, transcendentals=0),
        name="attend",
    )(lengths, q, k_cache, v_cache, q, kn, vn, hidden, w_o)


def solution(mesh):
    def local_step(hidden, ln_gain, ln_bias, w_q, w_k, w_v, w_o, k_cache, v_cache, lengths):
        half = D // 4
        inv = 10000.0 ** (-2.0 * jnp.arange(half, dtype=F32) / (D // 2))
        ang = lengths.astype(F32)[:, None] * inv
        cos, sin = jnp.cos(ang), jnp.sin(ang)
        zero = jnp.zeros_like(sin)
        cos_t = jnp.concatenate([cos, cos, jnp.ones((ROWS, 2 * half), F32)], axis=1)
        s1_t = jnp.concatenate([-sin, zero, zero, zero], axis=1)
        s2_t = jnp.concatenate([zero, sin, zero, zero], axis=1)
        q, kn, vn = project(hidden, ln_gain.reshape(1, DM), ln_bias.reshape(1, DM), cos_t, s1_t, s2_t, w_q, w_k, w_v)
        out = attend(lengths, q.reshape(2, 2, OWN * G, D),
                     k_cache.reshape(2, 2, OWN, 512, D), v_cache.reshape(2, 2, OWN, 512, D),
                     kn.reshape(2, 2, OWN * KV, D), vn.reshape(2, 2, OWN * KV, D),
                     hidden.reshape(2, 2, OWN, DM), w_o)
        return out.reshape(ROWS, DM), kn.reshape(ROWS, KV, D), vn.reshape(ROWS, KV, D)

    row_spec = P('dp', None)
    cache_spec = P('dp', 'sp', 'tp', None)
    head_spec = P('dp', 'tp', None)
    return jax.shard_map(local_step, mesh=mesh, in_specs=(row_spec, P(None), P(None), P(None, 'tp'), P(None, 'tp'), P(None, 'tp'), P('tp', None), cache_spec, cache_spec, P('dp')), out_specs=(row_spec, head_spec, head_spec), check_vma=False)
```

time: 672 us -> 243 us (0.36); the launches traced: 663 us -> 242 us
  waiting for transfers between devices: 346 us -> 0 us
  Pallas kernels: 0 us -> 231 us
  matrix products: 127 us -> 0 us
  other arithmetic: 85.6 us -> 1.89 us
  local copies, waits for them, and re-layouts: 88.5 us -> 8.48 us
  between operations: 14.9 us -> 0.69 us
    pallas_call x0 -> x2, Pallas kernels: none -> 231 us  [the longest x1 192 us: attend(): pl.pallas_call(functools.partial(attn_kernel, schedule()), grid=(NSTEP +...]
    psum x1 -> x0, waiting for transfers between devices: 188 us -> none  [local_step(): summed = lax.psum(partial_out, 'tp')]
    all_gather x1 -> x0, waiting for transfers between devices: 158 us -> none  [local_step(): gathered = lax.all_gather(packed, 'sp', axis=0)]
    dot_general x7 -> x0, matrix products: 127 us -> none  [the longest x1 42.9 us: local_step(): jnp.einsum('bkgd,bskd->bkgs', queries, k_cache, preferred_element_type=jn...]
    reduce_sum x5 -> x0, other arithmetic: 38.4 us -> none  [the longest x1 20.9 us: local_step(): jnp.sum(gathered[..., :head_dim] * factor[..., None], axis=0)]
    all_gather x1 -> x0, local copies, waits for them, and re-layouts: 33.2 us -> none  [local_step(): gathered = lax.all_gather(packed, 'sp', axis=0)]
    unnamed x43 -> x3, local copies, waits for them, and re-layouts: 29.5 us -> 6.88 us
    convert_element_type x5 -> x1, other arithmetic: 17.1 us -> 0.69 us  [local_step(): ang = lengths.astype(F32)[:, None] * inv]
  transfers between devices with their start and end apart: 2 -> 0, of which waited for: 2 -> 0; matrix products, arithmetic and copies ran while one was open for 0% -> 0% of each run, Pallas kernels for 0% -> 0%
where the time goes in v1:
time: 243 us; the launch traced here: 242 us
  Pallas kernels  231 us (95%)
  local copies, waits for them, and re-layouts  8.48 us (3%)
    pallas_call x1, Pallas kernels, attend(): pl.pallas_call(functools.partial(attn_kernel, schedule()), grid=(NSTEP +...  192 us
    pallas_call x1, Pallas kernels, project(): pl.pallas_call(qkv_kernel, grid=(8,), out_shape=(jax.ShapeDtypeStruct((RO...  38.8 us
    unnamed x3, local copies, waits for them, and re-layouts  6.88 us

profile of v1, /device:TPU:0, one launch (start us, length us, event | category | flops | bytes accessed | tf_op | source)
XLA Modules:
  0.0 242.2 jit_solution(7057319476209052323)
XLA Ops:
  0.6 0.1 pad.6.clone
  0.7 0.1 pad.3.clone
  0.8 0.7 convert_element_type.3
  1.5 0.7 reshape.45.g_ref
  2.2 0.7 reshape.46.b_ref
  2.9 1.0 multiply_sine_fusion
  3.9 0.2 maximum_maximum_fusion
  4.2 0.0 copy-start
  4.2 2.2 copy-done
  6.4 38.8 %qkv.1 = (f32[12288,128]{1,0:T(8,128)}, bf16[2048,128]{1,0:T(8,128)(2,1)}, bf16[2048,128]{1,0:T(8,128)(2,1)}) custom-call(bf16[512,4096]{1,0:T(8,128)(2,1)S(1)} %copy-done, bf16[1,4096]{1,0:T(2,128)(2,1)S(1)} %reshape.45.g_ref, bf16[1,4096]{1,0:T(2,128)(2,1)S(1)} %reshape.46.b_ref, f32[512,128]{1,0:T(8,128)S(1)} %get-tuple-element.12.cos_ref, ...), custom_call_target="tpu_custom_call" | custom-call | flops 17179869184 | bytes 50331648 | tf_op jit(solution)/shard_map/qkv/pallas_call | solution.py:110
  45.2 192.3 %attend.1 = bf16[4,128,4096]{2,1,0:T(8,128)(2,1)} custom-call(s32[512]{0:T(512)} %lens_ref.1, f32[2,2,3072,128]{3,2,1,0:T(8,128)} %bitcast.10, bf16[2,2,128,512,128]{4,3,2,1,0:T(8,128)(2,1)} %bitcast.1.k_ref, bf16[2,2,128,512,128]{4,3,2,1,0:T(8,128)(2,1)} %bitcast.2.v_ref, f32[2,2,3072,128]{3,2,1,0:T(8,128)} %bitcast.11, bf16[2,2,512,128]{3,2,1,0:T(8,128)(2,1)} %bitcast.13, ...), custom_call_target="tpu_custom_call" | custom-call | flops 10000000000 | bytes 178257920 | tf_op jit(solution)/shard_map/attend/pallas_call | solution.py:387
  237.5 4.7 %copy.14 = bf16[512,4096]{1,0:T(8,128)(2,1)} copy(bf16[512,4096]{1,0:T(8,128)(2,1)} %bitcast.12) | data formatting | bytes 8388608
  (6 shorter events, 0.0 us)
Async XLA Ops:
  4.2 2.2 copy-start

commit v2 on v1

--- a/solution.py
+++ b/solution.py
@@ -15,7 +15,7 @@
 OWN = 128
 STEP = 4
 NSTEP = OWN // STEP
-NCH = 4
+NCH = 8
 CR = OWN // NCH
 SPC = NSTEP // NCH
 HALF = DM // 2
@@ -25,7 +25,9 @@
 F32 = jnp.float32
 BF16 = jnp.bfloat16
 
-(KD, KDS, KX, KXS, KY, KFX, KFY, KFC, KGY, KGCX, KGCY, KGCD) = range(12)
+(KD, KDS, KX, KXS, KC, KY, KFX, KFY, KFC, KGY, KGCX, KGCY, KGCD) = range(13)
+NKIND = 13
+NP = CR // 2
 
 
 def qkv_kernel(h_ref, g_ref, b_ref, cos_ref, s1_ref, s2_ref, wq_ref, wk_ref, wv_ref,
@@ -124,8 +126,8 @@
 
 
 def attn_kernel(events, lens_ref, q_ref, k_ref, v_ref, qh_ref, kn_ref, vn_ref, hid_ref, wo_ref, out_ref,
-                pos, acc, st, drecv, dst, cst, xrecv, xst, pout, yrecv, obuf, wo, qown, knb, vnb, knf, vnf, hid,
-                ctxf, lhs, stage, lsem, osem, ssem, rsem):
+                pos, acc, st, drecv, dst, cst, sst, xrecv, xst, pout, yrecv, obuf, wo, qown, knb, vnb, knf, vnf, hid,
+                ctxf, lhs, stage, scr, sms, lsem, osem, ssem, rsem):
     i = pl.program_id(0)
     dp = lax.axis_index("dp")
     y = lax.axis_index("tp")
@@ -136,8 +138,7 @@
     dev_c = (dp, y, 2 * x + nc)
     dev_x = (dp, y, 2 * nx + c)
     dev_y = (dp, ny, s)
-    own = 2 * x + c
-    own_x = 2 * nx + c
+    own, own_x, own_y, own_xy = 2 * x + y, 2 * nx + y, 2 * x + ny, 2 * nx + ny
     base = s * 128
 
     def remote(kind, ch, src, dst_, dev):
@@ -145,7 +146,7 @@
                                             device_id=dev, device_id_type=MESH)
 
     locals_ = [
-        (wo_ref, wo), (qh_ref.at[x, c], qown), (kn_ref.at[x, c], knb), (vn_ref.at[x, c], vnb), (hid_ref.at[x, c], hid),
+        (wo_ref.at[:, pl.ds(pl.multiple_of(c * HALF, HALF), HALF)], wo), (qh_ref.at[x, c], qown), (kn_ref.at[x, c], knb), (vn_ref.at[x, c], vnb), (hid_ref.at[x, y, :, pl.ds(pl.multiple_of(c * HALF, HALF), HALF)], hid),
     ]
 
     def local_copy(n):
@@ -157,8 +158,6 @@
         sem = pltpu.get_barrier_semaphore()
         for dev in (dev_c, dev_x, dev_y):
             pl.semaphore_signal(sem, inc=1, device_id=dev, device_id_type=MESH)
-        for n in range(len(locals_)):
-            local_copy(n).start()
         col = lax.broadcasted_iota(jnp.int32, (48, 512), 1)
         row = lax.broadcasted_iota(jnp.int32, (48, 512), 0)
         jj = jnp.where(row >= G, row - G, row)
@@ -166,17 +165,19 @@
         pos[...] = jnp.where((col & 3) == head, col >> 2, 1 << 20)
         pl.semaphore_wait(sem, 3)
 
+    @pl.when(i == 1)
+    def _():
+        for n in range(len(locals_)):
+            local_copy(n).start()
+
     lane = lax.broadcasted_iota(jnp.int32, (48, D), 1)
     low = lax.broadcasted_iota(jnp.int32, (48, D), 0) < G
     low1 = lax.broadcasted_iota(jnp.int32, (48, 1), 0) < G
 
     @pl.when(i < NSTEP)
     def _():
-        ch = i // SPC
-        within = lax.rem(i, SPC)
         for xo in range(2):
             for co in range(2):
-                stats = jnp.where(within == 0, 0.0, st[ch, co, xo])
                 for pp in range(STEP // 2):
                     q48 = q_ref[xo, co, pp * 48:(pp + 1) * 48, :]
                     qbd = jnp.concatenate([jnp.where(low, q48, 0.0), jnp.where(low, 0.0, q48)], axis=1).astype(BF16)
@@ -184,7 +185,17 @@
                     sc = lax.dot_general(qbd, kk, (((1,), (1,)), ((), ())), preferred_element_type=F32)
                     r0 = (2 * xo + co) * OWN + i * STEP + 2 * pp
                     lenv = jnp.where(low1, lens_ref[r0] - base, lens_ref[r0 + 1] - base)
-                    sc = jnp.where(pos[...] < lenv, sc * SCALE2, NEG)
+                    scr[(xo * 2 + co) * (STEP // 2) + pp] = jnp.where(pos[...] < lenv, sc * SCALE2, NEG)
+
+    @pl.when(i < NSTEP)
+    def _():
+        ch = i // SPC
+        within = lax.rem(i, SPC)
+        for xo in range(2):
+            for co in range(2):
+                stats = jnp.where(within == 0, 0.0, st[ch, co, xo])
+                for pp in range(STEP // 2):
+                    sc = scr[(xo * 2 + co) * (STEP // 2) + pp]
                     m = jnp.maximum(jnp.max(sc, axis=1, keepdims=True), FLOOR)
                     w = jnp.exp2(sc - m)
                     l = jnp.sum(w, axis=1, keepdims=True)
@@ -194,13 +205,14 @@
                     acc[co, xo, pl.ds(at, G), :] = o[:G, :D]
                     acc[co, xo, pl.ds(at + G, G), :] = o[G:, D:]
                     idx = within * (STEP // 2) + pp
-                    stats = jnp.where(lane == idx, m, jnp.where(lane == idx + 64, l, stats))
+                    stats = jnp.where(lane == idx, m, jnp.where(lane == idx + NP, l, stats))
                 st[ch, co, xo] = stats
 
     def pick(block, n):
-        m = jnp.sum(jnp.where(lane == n, block, 0.0), axis=1, keepdims=True)
-        l = jnp.sum(jnp.where(lane == n + 64, block, 0.0), axis=1, keepdims=True)
-        return m, l
+        return jnp.sum(jnp.where(lane == n, block, 0.0), axis=1, keepdims=True)
+
+    def sums(block):
+        return pltpu.roll(block, D - NP, 1)
 
     def crows(ch):
         return pl.ds(ch * CR * G, CR * G)
@@ -215,84 +227,113 @@
         return remote(KX, ch, acc.at[c, nx, crows(ch)], xrecv.at[crows(ch)], dev_x)
 
     def x_st(ch):
-        return remote(KXS, ch, cst.at[ch, nx], xst.at[ch], dev_x)
+        return remote(KXS, ch, sst.at[ch], xst.at[ch], dev_x)
 
     def y_part(ch):
-        return remote(KY, ch, pout.at[ch, ny], yrecv.at[ch], dev_y)
+        return remote(KY, ch, pout.at[ch % 4, ny], yrecv.at[ch], dev_y)
+
+    def ctx_copy(ch):
+        return remote(KC, ch, ctxf.at[ch, c], ctxf.at[ch, c], dev_c)
+
+    def ctx_in(ch):
+        return remote(KC, ch, ctxf.at[ch, nc], ctxf.at[ch, nc], dev_c)
 
     def piece(half, owner, ch):
         return obuf.at[half, owner, pl.ds(ch * CR, CR)]
 
     def gather(kind, ch, dev, half, owner):
         return remote(kind, ch, piece(half, owner, ch), piece(half, owner, ch), dev)
-
-    own_c = 2 * x + nc
-    own_xc = 2 * nx + nc
 
     def ev_core(ch):
         c_acc(ch).start()
         c_st(ch).start()
 
+    def pairs(ch, body, init):
+        def four(t, carry):
+            for u in range(4):
+                n = t * 4 + u
+                rows = pl.ds(pl.multiple_of((ch * CR + 2 * n) * G, 2 * G), 2 * G)
+                carry = body(n, rows, carry)
+            return carry
+        return lax.fori_loop(0, CR // 8, four, init)
+
+    def spread(ref, ch, n):
+        krows = pl.ds(pl.multiple_of((ch * CR + 2 * n) * KV, 2 * KV), 2 * KV)
+        rr = lax.broadcasted_iota(jnp.int32, (48, 8), 0)
+        cc = lax.broadcasted_iota(jnp.int32, (48, 8), 1)
+        hot = ((rr >= cc * 6) & (rr < cc * 6 + 6)).astype(F32)
+        return jnp.dot(hot, ref[krows, :], preferred_element_type=F32)
+
     def ev_x(ch):
         c_acc(ch).wait_recv()
         c_st(ch).wait_recv()
 
-        def merge(xo, order):
-            mine = st[ch, c, xo]
-            theirs = dst[ch, xo]
-
-            def body(n, out):
-                rows = pl.ds(pl.multiple_of((ch * CR + 2 * n) * G, 2 * G), 2 * G)
-                ma, la = pick(mine, n)
-                mb, lb = pick(theirs, n)
-                m = jnp.maximum(ma, mb)
-                fa, fb = jnp.exp2(ma - m), jnp.exp2(mb - m)
-                acc[c, xo, rows, :] = acc[c, xo, rows, :] * fa + drecv[xo, rows, :] * fb
-                return jnp.where(lane == n, m, jnp.where(lane == n + 64, la * fa + lb * fb, out))
-            cst[ch, xo] = lax.fori_loop(0, CR // 2, body, jnp.zeros((48, D), F32))
-        merge(nx, 0)
+        def merge(xo):
+            a, b = st[ch, c, xo], dst[ch, xo]
+            m = jnp.maximum(a, b)
+            fa, fb = jnp.exp2(a - m), jnp.exp2(b - m)
+            both = jnp.where(lane < NP, m, pltpu.roll(sums(a) * fa + sums(b) * fb, NP, 1))
+            if xo is x:
+                cst[ch] = both
+            else:
+                small = both[:8]
+                for g in range(1, 6):
+                    small = jnp.where(lane[:8] >= 16 * g, pltpu.roll(both[8 * g:8 * g + 8], 16 * g, 1), small)
+                sst[ch] = small
+
+            def body(n, rows, carry):
+                acc[c, xo, rows, :] = acc[c, xo, rows, :] * pick(fa, n) + drecv[xo, rows, :] * pick(fb, n)
+                return carry
+            pairs(ch, body, 0)
+        merge(nx)
         x_acc(ch).start()
         x_st(ch).start()
-        merge(x, 1)
-
-    def ev_proj(ch):
+        merge(x)
+
+    def ev_self(ch):
         if ch == 0:
             for n in range(len(locals_)):
                 local_copy(n).wait()
             knf[...] = knb[...].astype(F32)
             vnf[...] = vnb[...].astype(F32)
+
+        def body(n, rows, out):
+            val = jnp.sum(qown[rows, :].astype(BF16).astype(F32) * spread(knf, ch, n), axis=1, keepdims=True)
+            return jnp.where(lane == n, val, out)
+        sms[ch] = pairs(ch, body, jnp.zeros((48, D), F32)) * SCALE2
+
+    def ev_ctx(ch):
         x_acc(ch).wait_recv()
         x_st(ch).wait_recv()
-        mine = cst[ch, x]
-        theirs = xst[ch]
-        rr = lax.broadcasted_iota(jnp.int32, (48, 8), 0)
-        cc = lax.broadcasted_iota(jnp.int32, (48, 8), 1)
-        spread = ((rr >= cc * 6) & (rr < cc * 6 + 6)).astype(F32)
-
-        def body(n, _):
-            rows = pl.ds(pl.multiple_of((ch * CR + 2 * n) * G, 2 * G), 2 * G)
-            krows = pl.ds(pl.multiple_of((ch * CR + 2 * n) * KV, 2 * KV), 2 * KV)
-            kx = jnp.dot(spread, knf[krows, :], preferred_element_type=F32)
-            vx = jnp.dot(spread, vnf[krows, :], preferred_element_type=F32)
-            ms = jnp.sum(qown[rows, :].astype(BF16).astype(F32) * kx, axis=1, keepdims=True) * SCALE2
-            ma, la = pick(mine, n)
-            mb, lb = pick(theirs, n)
-            m = jnp.maximum(jnp.maximum(ma, mb), ms)
-            fa, fb, fs = jnp.exp2(ma - m), jnp.exp2(mb - m), jnp.exp2(ms - m)
-            tot = la * fa + lb * fb + fs
-            ctx = acc[c, x, rows, :] * fa + xrecv[rows, :] * fb + fs * vx
-            ctxf[pl.ds(pl.multiple_of(n * 48, 48), 48), :] = ctx / tot
-            return 0
-        lax.fori_loop(0, CR // 2, body, 0)
+        a, z, got = cst[ch], sms[ch], xst[ch]
+        b = jnp.concatenate([got] + [pltpu.roll(got, D - 16 * g, 1) for g in range(1, 6)], axis=0)
+        m = jnp.maximum(jnp.maximum(a, b), z)
+        fa, fb, fs = jnp.exp2(a - m), jnp.exp2(b - m), jnp.exp2(z - m)
+        tot = sums(a) * fa + sums(b) * fb + fs
+        fa, fb, fs = fa / tot, fb / tot, fs / tot
+
+        def body(n, rows, carry):
+            ctx = acc[c, x, rows, :] * pick(fa, n) + xrecv[rows, :] * pick(fb, n) + pick(fs, n) * spread(vnf, ch, n)
+            ctxf[ch, c, pl.ds(pl.multiple_of(n * 48, 48), 48), :] = ctx
+            return carry
+        pairs(ch, body, 0)
+        ctx_copy(ch).start()
+
+    def ev_proj(ch):
+        ctx_in(ch).wait_recv()
         for j in range(G):
-            lhs[:, j * D:(j + 1) * D] = ctxf[pl.ds(j, CR, G), :].astype(BF16)
-
-        for half in range(2):
-            def mm(n, _, half=half):
-                cols = pl.ds(pl.multiple_of(half * HALF + n * 512, 512), 512)
-                pout[ch, half, :, pl.ds(pl.multiple_of(n * 512, 512), 512)] = jnp.dot(lhs[...], wo[:, cols], preferred_element_type=F32)
-                return 0
-            lax.fori_loop(0, HALF // 512, mm, 0)
+            for half in range(2):
+                lhs[half * CR:(half + 1) * CR, j * D:(j + 1) * D] = ctxf[ch, half, pl.ds(j, CR, G), :].astype(BF16)
+
+        def mm(n, _):
+            cols = pl.ds(pl.multiple_of(n * 512, 512), 512)
+            part = jnp.dot(lhs[...], wo[:, cols], preferred_element_type=F32)
+            pout[ch % 4, 0, :, cols] = part[:CR]
+            pout[ch % 4, 1, :, cols] = part[CR:]
+            return 0
+        if ch >= 4:
+            y_part(ch - 4).wait_send()
+        lax.fori_loop(0, HALF // 512, mm, 0)
         y_part(ch).start()
 
     def ev_sum(ch):
@@ -301,33 +342,32 @@
 
         def body(n, _):
             cols = pl.ds(pl.multiple_of(n * 512, 512), 512)
-            hcols = pl.ds(pl.multiple_of(y * HALF + n * 512, 512), 512)
-            obuf[y, own, rows, cols] = pout[ch, y, :, cols] + yrecv[ch, :, cols] + hid[rows, hcols].astype(F32)
+            obuf[c, own, rows, cols] = pout[ch % 4, y, :, cols] + yrecv[ch, :, cols] + hid[rows, cols].astype(F32)
             return 0
         lax.fori_loop(0, HALF // 512, body, 0)
-        gather(KFX, ch, dev_x, y, own).start()
-        gather(KFY, ch, dev_y, y, own).start()
-        gather(KFC, ch, dev_c, y, own).start()
+        gather(KFX, ch, dev_x, c, own).start()
+        gather(KFY, ch, dev_y, c, own).start()
+        gather(KFC, ch, dev_c, c, own).start()
 
     def ev_fwd(ch):
-        gather(KFX, ch, dev_x, y, own_x).wait_recv()
-        gather(KGY, ch, dev_y, y, own_x).start()
-        gather(KGCX, ch, dev_c, y, own_x).start()
-        gather(KFY, ch, dev_y, ny, own).wait_recv()
-        gather(KGCY, ch, dev_c, ny, own).start()
+        gather(KFX, ch, dev_x, c, own_x).wait_recv()
+        gather(KGY, ch, dev_y, c, own_x).start()
+        gather(KGCX, ch, dev_c, c, own_x).start()
+        gather(KFY, ch, dev_y, c, own_y).wait_recv()
+        gather(KGCY, ch, dev_c, c, own_y).start()
 
     def ev_last(ch):
-        gather(KGY, ch, dev_y, ny, own_x).wait_recv()
-        gather(KGCD, ch, dev_c, ny, own_x).start()
+        gather(KGY, ch, dev_y, c, own_xy).wait_recv()
+        gather(KGCD, ch, dev_c, c, own_xy).start()
 
     def out_copy(ch):
         return pltpu.make_async_copy(stage.at[ch % 2], out_ref.at[:, pl.ds(ch * CR, CR)], osem.at[ch % 2])
 
     def ev_out(ch):
-        gather(KFC, ch, dev_c, y, own_c).wait_recv()
-        gather(KGCX, ch, dev_c, y, own_xc).wait_recv()
-        gather(KGCY, ch, dev_c, ny, own_c).wait_recv()
-        gather(KGCD, ch, dev_c, ny, own_xc).wait_recv()
+        gather(KFC, ch, dev_c, nc, own).wait_recv()
+        gather(KGCX, ch, dev_c, nc, own_x).wait_recv()
+        gather(KGCY, ch, dev_c, nc, own_y).wait_recv()
+        gather(KGCD, ch, dev_c, nc, own_xy).wait_recv()
         if ch >= 2:
             out_copy(ch - 2).wait()
         rows = pl.ds(ch * CR, CR)
@@ -345,14 +385,16 @@
         c_st(ch).wait_send()
         x_acc(ch).wait_send()
         x_st(ch).wait_send()
-        y_part(ch).wait_send()
-        for kind, dev, half, owner in ((KFX, dev_x, y, own), (KFY, dev_y, y, own), (KFC, dev_c, y, own), (KGY, dev_y, y, own_x),
-                                       (KGCX, dev_c, y, own_x), (KGCY, dev_c, ny, own), (KGCD, dev_c, ny, own_x)):
-            gather(kind, ch, dev, half, owner).wait_send()
+        ctx_copy(ch).wait_send()
+        if ch >= NCH - 4:
+            y_part(ch).wait_send()
+        for kind, dev, owner in ((KFX, dev_x, own), (KFY, dev_y, own), (KFC, dev_c, own), (KGY, dev_y, own_x),
+                                 (KGCX, dev_c, own_x), (KGCY, dev_c, own_y), (KGCD, dev_c, own_xy)):
+            gather(kind, ch, dev, c, owner).wait_send()
         if ch >= NCH - 2:
             out_copy(ch).wait()
 
-    table = {"core": ev_core, "x": ev_x, "proj": ev_proj, "sum": ev_sum, "fwd": ev_fwd, "last": ev_last, "out": ev_out, "drain": ev_drain}
+    table = {"core": ev_core, "x": ev_x, "self": ev_self, "ctx": ev_ctx, "proj": ev_proj, "sum": ev_sum, "fwd": ev_fwd, "last": ev_last, "out": ev_out, "drain": ev_drain}
     for when, names in events:
         @pl.when(i == when)
         def _(names=names):
@@ -361,7 +403,7 @@
 
 
 def schedule():
-    offs = (("core", 0), ("x", 2), ("proj", 10), ("sum", 16), ("fwd", 20), ("last", 23), ("out", 25))
+    offs = (("core", 0), ("x", 1), ("self", 2), ("ctx", 6), ("proj", 7), ("sum", 10), ("fwd", 14), ("last", 17), ("out", 19))
     order = {name: n for n, (name, _) in enumerate(offs)}
     plan = {}
     for ch in range(NCH):
@@ -398,26 +440,29 @@
             pltpu.VMEM((NCH, 2, 2, 48, D), F32),
             pltpu.VMEM((2, OWN * G, D), F32),
             pltpu.VMEM((NCH, 2, 48, D), F32),
-            pltpu.VMEM((NCH, 2, 48, D), F32),
+            pltpu.VMEM((NCH, 48, D), F32),
+            pltpu.VMEM((NCH, 8, D), F32),
             pltpu.VMEM((OWN * G, D), F32),
-            pltpu.VMEM((NCH, 48, D), F32),
-            pltpu.VMEM((NCH, 2, CR, HALF), F32),
+            pltpu.VMEM((NCH, 8, D), F32),
+            pltpu.VMEM((4, 2, CR, HALF), F32),
             pltpu.VMEM((NCH, CR, HALF), F32),
             pltpu.VMEM((2, 4, OWN, HALF), F32),
-            pltpu.VMEM((G * D, DM), BF16),
+            pltpu.VMEM((G * D, HALF), BF16),
             pltpu.VMEM((OWN * G, D), F32),
             pltpu.VMEM((OWN * KV, D), BF16),
             pltpu.VMEM((OWN * KV, D), BF16),
             pltpu.VMEM((OWN * KV, D), F32),
             pltpu.VMEM((OWN * KV, D), F32),
-            pltpu.VMEM((OWN, DM), BF16),
-            pltpu.VMEM((CR * G, D), F32),
-            pltpu.VMEM((CR, G * D), BF16),
+            pltpu.VMEM((OWN, HALF), BF16),
+            pltpu.VMEM((NCH, 2, CR * G, D), F32),
+            pltpu.VMEM((2 * CR, G * D), BF16),
             pltpu.VMEM((2, 4, CR, DM), BF16),
+            pltpu.VMEM((2 * STEP, 48, 512), F32),
+            pltpu.VMEM((NCH, 48, D), F32),
             pltpu.SemaphoreType.DMA((5,)),
             pltpu.SemaphoreType.DMA((2,)),
-            pltpu.SemaphoreType.DMA((12, NCH)),
-            pltpu.SemaphoreType.DMA((12, NCH)),
+            pltpu.SemaphoreType.DMA((NKIND, NCH)),
+            pltpu.SemaphoreType.DMA((NKIND, NCH)),
         ],
         compiler_params=pltpu.CompilerParams(vmem_limit_bytes=67043328, collective_id=0, has_side_effects=True,
                                              dimension_semantics=("arbitrary",)),

time: 243 us -> 178 us (0.73)
  Pallas kernels: 231 us -> 167 us
    pallas_call x1, Pallas kernels: 192 us -> 128 us  [attend(): pl.pallas_call(functools.partial(attn_kernel, schedule()), grid=(NSTEP +...]
where the time goes in v2:
time: 178 us
  Pallas kernels  167 us (94%)
  local copies, waits for them, and re-layouts  8.48 us (5%)
  other arithmetic  1.89 us (1%)
    pallas_call x1, Pallas kernels, attend(): pl.pallas_call(functools.partial(attn_kernel, schedule()), grid=(NSTEP +...  128 us
    pallas_call x1, Pallas kernels, project(): pl.pallas_call(qkv_kernel, grid=(8,), out_shape=(jax.ShapeDtypeStruct((RO...  38.8 us
    unnamed x3, local copies, waits for them, and re-layouts  6.88 us

profile of v2, /device:TPU:0, one launch (start us, length us, event | category | flops | bytes accessed | tf_op | source)
XLA Modules:
  0.0 177.7 jit_solution(9590670549613202361)
XLA Ops:
  0.6 0.1 pad.6.clone
  0.7 0.1 pad.3.clone
  0.8 0.7 convert_element_type.3
  1.5 0.7 reshape.45.g_ref
  2.2 0.7 reshape.46.b_ref
  2.9 1.0 multiply_sine_fusion
  3.9 0.2 maximum_maximum_fusion
  4.2 0.0 copy-start
  4.2 2.2 %copy-done = bf16[512,4096]{1,0:T(8,128)(2,1)S(1)} copy-done((bf16[512,4096]{1,0:T(8,128)(2,1)S(1)}, bf16[512,4096]{1,0:T(8,128)(2,1)}, u32[]{:S(2)}) %copy-start) | copy-done | bytes 4194328
  6.4 38.8 %qkv.1 = (f32[12288,128]{1,0:T(8,128)}, bf16[2048,128]{1,0:T(8,128)(2,1)}, bf16[2048,128]{1,0:T(8,128)(2,1)}) custom-call(bf16[512,4096]{1,0:T(8,128)(2,1)S(1)} %copy-done, bf16[1,4096]{1,0:T(2,128)(2,1)S(1)} %reshape.45.g_ref, bf16[1,4096]{1,0:T(2,128)(2,1)S(1)} %reshape.46.b_ref, f32[512,128]{1,0:T(8,128)S(1)} %get-tuple-element.12.cos_ref, ...), custom_call_target="tpu_custom_call" | custom-call | flops 17179869184 | bytes 50331648 | tf_op jit(solution)/shard_map/qkv/pallas_call | solution.py:112
  45.2 127.8 %attend.1 = bf16[4,128,4096]{2,1,0:T(8,128)(2,1)} custom-call(s32[512]{0:T(512)} %lens_ref.1, f32[2,2,3072,128]{3,2,1,0:T(8,128)} %bitcast.10, bf16[2,2,128,512,128]{4,3,2,1,0:T(8,128)(2,1)} %bitcast.1.k_ref, bf16[2,2,128,512,128]{4,3,2,1,0:T(8,128)(2,1)} %bitcast.2.v_ref, f32[2,2,3072,128]{3,2,1,0:T(8,128)} %bitcast.11, bf16[2,2,512,128]{3,2,1,0:T(8,128)(2,1)} %bitcast.13, ...), custom_call_target="tpu_custom_call" | custom-call | flops 10000000000 | bytes 178257920 | tf_op jit(solution)/shard_map/attend/pallas_call | solution.py:429
  173.0 4.7 %copy.14 = bf16[512,4096]{1,0:T(8,128)(2,1)} copy(bf16[512,4096]{1,0:T(8,128)(2,1)} %bitcast.12) | data formatting | bytes 8388608
  (6 shorter events, 0.0 us)
Async XLA Ops:
  4.2 2.2 %copy-start = (bf16[512,4096]{1,0:T(8,128)(2,1)S(1)}, bf16[512,4096]{1,0:T(8,128)(2,1)}, u32[]{:S(2)}) copy-start(bf16[512,4096]{1,0:T(8,128)(2,1)} %h_ref.1) | copy-start | bytes 12582916

commit v3 on v2

--- a/solution.py
+++ b/solution.py
@@ -18,6 +18,10 @@
 NCH = 8
 CR = OWN // NCH
 SPC = NSTEP // NCH
+NBUF = 3
+XFWD = (0, 3, 6)
+GROUPS = ((0, 1), (2, 3), (4, 5), (6, 7))
+OFFS = {'core': 0, 'x': 1.0, 'self': 4.5, 'ctx': 5.5, 'proj': 8.0, 'sum': 14.5, 'fwd': 19.0, 'last': 28.5, 'out': 42.0}
 HALF = DM // 2
 NEG = -3e38
 FLOOR = -1e38
@@ -30,104 +34,141 @@
 NP = CR // 2
 
 
-def qkv_kernel(h_ref, g_ref, b_ref, cos_ref, s1_ref, s2_ref, wq_ref, wk_ref, wv_ref,
-               q_ref, k_ref, v_ref, hn, wbuf, res, kvf, sems):
+def qkv_kernel(h_ref, gb_ref, cos_ref, s1_ref, s2_ref, wq_ref, wk_ref, wv_ref,
+               q_ref, k_ref, v_ref, hid, hn, wbuf, res, tb, kvr, kvf, sems, ksem, hsem, qsem, ssem, rsem):
     i = pl.program_id(0)
-    nq = 6
-
-    def fetch(t, slot):
-        @pl.when(t < nq)
-        def _():
-            pltpu.make_async_copy(wq_ref.at[:, pl.ds(pl.multiple_of(t * 512, 512), 512)], wbuf.at[slot], sems.at[slot]).start()
-
-        @pl.when(t == nq)
-        def _():
-            pltpu.make_async_copy(wk_ref, wbuf.at[slot], sems.at[slot]).start()
-
-        @pl.when(t == nq + 1)
-        def _():
-            pltpu.make_async_copy(wv_ref, wbuf.at[slot], sems.at[slot]).start()
-
-    @pl.when(i == 0)
-    def _():
-        fetch(i, 0)
-        gain = 1.0 + g_ref[...].astype(F32)
-        bias = b_ref[...].astype(F32)
-
-        def norm(r, _):
-            rows = pl.ds(pl.multiple_of(r * 16, 16), 16)
-            wide = h_ref[rows, :].astype(F32)
+    rb = 128
+    dp, y, s = lax.axis_index("dp"), lax.axis_index("tp"), lax.axis_index("sp")
+    c = lax.rem(s, 2)
+    nc = 1 - c
+    peer = (dp, y, s - c + nc)
+
+    def fetch_kv():
+        cols = pl.ds(pl.multiple_of(c * 256, 256), 256)
+        return (pltpu.make_async_copy(wk_ref.at[:, cols], wbuf.at[0, :, pl.ds(0, 256)], ksem.at[0]),
+                pltpu.make_async_copy(wv_ref.at[:, cols], wbuf.at[0, :, pl.ds(256, 256)], ksem.at[1]))
+
+    def fetch_q(t):
+        cols = pl.ds(pl.multiple_of((3 * c + t - 1) * 512, 512), 512)
+        return pltpu.make_async_copy(wq_ref.at[:, cols], wbuf.at[lax.rem(t, 2)], sems.at[lax.rem(t, 2)])
+
+    def hcopy(r):
+        rows = pl.ds(r * rb, rb)
+        return pltpu.make_async_copy(h_ref.at[rows], hid.at[rows], hsem.at[r])
+
+    def send(t):
+        dst = kvr if t == 0 else q_ref.at[3 * c + t - 1]
+        return pltpu.make_async_remote_copy(src_ref=tb.at[t], dst_ref=dst, send_sem=ssem.at[t], recv_sem=rsem.at[t],
+                                            device_id=peer, device_id_type=MESH)
+
+    def incoming(t):
+        dst = kvr if t == 0 else q_ref.at[3 * nc + t - 1]
+        return pltpu.make_async_remote_copy(src_ref=tb.at[t], dst_ref=dst, send_sem=ssem.at[t], recv_sem=rsem.at[t],
+                                            device_id=peer, device_id_type=MESH)
+
+    def keep(t):
+        return pltpu.make_async_copy(tb.at[t], q_ref.at[3 * c + t - 1], qsem.at[t])
+
+    def norm(r):
+        for u in range(rb // 16):
+            rows = pl.ds(r * rb + u * 16, 16)
+            wide = hid[rows, :].astype(F32)
             mean = jnp.mean(wide, axis=1, keepdims=True)
             cen = wide - mean
             var = jnp.mean(cen * cen, axis=1, keepdims=True)
-            hn[rows, :] = ((cen * lax.rsqrt(var + 1e-5)) * gain + bias).astype(BF16)
-            return 0
-        lax.fori_loop(0, ROWS // 16, norm, 0)
-
-    slot = lax.rem(i, 2)
-
-    @pl.when(i < nq + 1)
-    def _():
-        fetch(i + 1, 1 - slot)
-    pltpu.make_async_copy(wk_ref, wbuf.at[slot], sems.at[slot]).wait()
-    res[...] = jnp.dot(hn[...], wbuf[slot], preferred_element_type=F32)
+            hn[rows, :] = ((cen * lax.rsqrt(var + 1e-5)) * gb_ref[0:1, :] + gb_ref[1:2, :]).astype(BF16)
 
     def rope(x, rows):
         return x * cos_ref[rows, :] + pltpu.roll(x, 96, 1) * s1_ref[rows, :] + pltpu.roll(x, 32, 1) * s2_ref[rows, :]
 
-    @pl.when(i < nq)
-    def _():
-        def body(r, _):
-            rows = pl.ds(pl.multiple_of(r * 64, 64), 64)
+    def finish(t, slot):
+        for r in range(ROWS // 64):
+            rows = pl.ds(r * 64, 64)
             for u in range(4):
-                x = rope(res[rows, u * D:(u + 1) * D], rows)
-                q_ref[pl.ds(r * (64 * G) + i * 4 + u, 64, G), :] = x
-            return 0
-        lax.fori_loop(0, ROWS // 64, body, 0)
-
-    @pl.when(i == nq)
-    def _():
-        def body(r, _):
-            rows = pl.ds(pl.multiple_of(r * 64, 64), 64)
-            for u in range(KV):
-                kvf[pl.ds(r * (64 * KV) + u, 64, KV), :] = rope(res[rows, u * D:(u + 1) * D], rows)
-            return 0
-        lax.fori_loop(0, ROWS // 64, body, 0)
-        k_ref[...] = kvf[...].astype(BF16)
-
-    @pl.when(i == nq + 1)
-    def _():
-        def body(r, _):
-            rows = pl.ds(pl.multiple_of(r * 64, 64), 64)
-            for u in range(KV):
-                kvf[pl.ds(r * (64 * KV) + u, 64, KV), :] = res[rows, u * D:(u + 1) * D]
-            return 0
-        lax.fori_loop(0, ROWS // 64, body, 0)
-        v_ref[...] = kvf[...].astype(BF16)
-
-
-def project(hidden, ln_gain, ln_bias, cos_t, s1_t, s2_t, w_q, w_k, w_v):
+                val = res[slot, rows, u * D:(u + 1) * D]
+                tb[t, pl.ds(r * 256 + u, 64, 4), :] = val if (t == 0 and u >= 2) else rope(val, rows)
+
+    def mul(t):
+        res[t % 2] = jnp.dot(hn[...], wbuf[t % 2], preferred_element_type=F32)
+
+    @pl.when(i == 0)
+    def _():
+        sem = pltpu.get_barrier_semaphore()
+        pl.semaphore_signal(sem, inc=1, device_id=peer, device_id_type=MESH)
+        hcopy(0).start()
+        for cp in fetch_kv():
+            cp.start()
+        for r in range(1, 4):
+            hcopy(r).start()
+        fetch_q(1).start()
+        hcopy(0).wait()
+        norm(0)
+        for cp in fetch_kv():
+            cp.wait()
+        for r in range(4):
+            if r < 3:
+                hcopy(r + 1).wait()
+            res[0, r * rb:(r + 1) * rb, :] = jnp.dot(hn[r * rb:(r + 1) * rb, :], wbuf[0], preferred_element_type=F32)
+            if r < 3:
+                norm(r + 1)
+        pl.semaphore_wait(sem, 1)
+
+    for t in range(1, 4):
+        @pl.when(i == t)
+        def _(t=t):
+            if t < 3:
+                fetch_q(t + 1).start()
+            fetch_q(t).wait()
+            finish(t - 1, (t - 1) % 2)
+            mul(t)
+            send(t - 1).start()
+            if t > 1:
+                keep(t - 1).start()
+
+    @pl.when(i == 4)
+    def _():
+        finish(3, 1)
+        send(3).start()
+        keep(3).start()
+        incoming(0).wait_recv()
+        for ref, off in ((k_ref, 0), (v_ref, 2)):
+            for u in range(2):
+                kvf[pl.ds(2 * c + u, ROWS, 4), :] = tb[0, pl.ds(off + u, ROWS, 4), :]
+                kvf[pl.ds(2 * nc + u, ROWS, 4), :] = kvr[pl.ds(off + u, ROWS, 4), :]
+            ref[...] = kvf[...].astype(BF16)
+        for t in range(1, 4):
+            keep(t).wait()
+            incoming(t).wait_recv()
+        for t in range(4):
+            send(t).wait_send()
+
+
+def project(hidden, gb, cos_t, s1_t, s2_t, w_q, w_k, w_v):
     vm = pl.BlockSpec(memory_space=pltpu.VMEM)
     hbm = pl.BlockSpec(memory_space=pl.ANY)
     return pl.pallas_call(
         qkv_kernel,
-        grid=(8,),
-        out_shape=(jax.ShapeDtypeStruct((ROWS * G, D), F32),
+        grid=(5,),
+        out_shape=(jax.ShapeDtypeStruct((6, ROWS * 4, D), F32),
                    jax.ShapeDtypeStruct((ROWS * KV, D), BF16),
                    jax.ShapeDtypeStruct((ROWS * KV, D), BF16)),
-        in_specs=[vm] * 6 + [hbm] * 3,
-        out_specs=(vm, vm, vm),
-        scratch_shapes=[pltpu.VMEM((ROWS, DM), BF16), pltpu.VMEM((2, DM, 512), BF16), pltpu.VMEM((ROWS, 512), F32),
-                        pltpu.VMEM((ROWS * KV, D), F32), pltpu.SemaphoreType.DMA((2,))],
-        compiler_params=pltpu.CompilerParams(vmem_limit_bytes=48 * 1024 * 1024, dimension_semantics=("arbitrary",)),
-        cost_estimate=pl.CostEstimate(flops=2 * ROWS * DM * 4096, bytes_accessed=48 << 20, transcendentals=0),
+        in_specs=[hbm] + [vm] * 4 + [hbm] * 3,
+        out_specs=(hbm, vm, vm),
+        scratch_shapes=[pltpu.VMEM((ROWS, DM), BF16), pltpu.VMEM((ROWS, DM), BF16), pltpu.VMEM((2, DM, 512), BF16),
+                        pltpu.VMEM((2, ROWS, 512), F32), pltpu.VMEM((4, ROWS * 4, D), F32), pltpu.VMEM((ROWS * 4, D), F32),
+                        pltpu.VMEM((ROWS * KV, D), F32),
+                        pltpu.SemaphoreType.DMA((2,)), pltpu.SemaphoreType.DMA((2,)), pltpu.SemaphoreType.DMA((4,)),
+                        pltpu.SemaphoreType.DMA((4,)), pltpu.SemaphoreType.DMA((4,)), pltpu.SemaphoreType.DMA((4,))],
+        compiler_params=pltpu.CompilerParams(vmem_limit_bytes=60 * 1024 * 1024, dimension_semantics=("arbitrary",),
+                                             collective_id=1, has_side_effects=True),
+        cost_estimate=pl.CostEstimate(flops=ROWS * DM * 4096, bytes_accessed=32 << 20, transcendentals=0),
         name="qkv",
-    )(hidden, ln_gain, ln_bias, cos_t, s1_t, s2_t, w_q, w_k, w_v)
-
-
-def attn_kernel(events, lens_ref, q_ref, k_ref, v_ref, qh_ref, kn_ref, vn_ref, hid_ref, wo_ref, out_ref,
-                pos, acc, st, drecv, dst, cst, sst, xrecv, xst, pout, yrecv, obuf, wo, qown, knb, vnb, knf, vnf, hid,
-                ctxf, lhs, stage, scr, sms, lsem, osem, ssem, rsem):
+    )(hidden, gb, cos_t, s1_t, s2_t, w_q, w_k, w_v)
+
+
+def attn_kernel(events, lens_ref, q_ref, kc_ref, vc_ref, qh_ref, kn_ref, vn_ref, hid_ref, wo_ref, out_ref,
+                kbuf, vbuf, pos, acc, st, drecv, dst, cst, sst, xrecv, xst, pout, yrecv, obuf, wo, qown, knb, vnb, knf, vnf, hid,
+                ctxf, lhs, stage, scr, sms, csem, lsem, osem, ssem, rsem):
     i = pl.program_id(0)
     dp = lax.axis_index("dp")
     y = lax.axis_index("tp")
@@ -146,12 +187,29 @@
                                             device_id=dev, device_id_type=MESH)
 
     locals_ = [
-        (wo_ref.at[:, pl.ds(pl.multiple_of(c * HALF, HALF), HALF)], wo), (qh_ref.at[x, c], qown), (kn_ref.at[x, c], knb), (vn_ref.at[x, c], vnb), (hid_ref.at[x, y, :, pl.ds(pl.multiple_of(c * HALF, HALF), HALF)], hid),
+        (wo_ref.at[:, pl.ds(pl.multiple_of(c * HALF, HALF), HALF)], wo), (qh_ref.at[:, x, c], qown), (kn_ref.at[x, c], knb), (vn_ref.at[x, c], vnb), (hid_ref.at[x, y, :, pl.ds(pl.multiple_of(c * HALF, HALF), HALF)], hid),
     ]
 
     def local_copy(n):
         a, b = locals_[n]
         return pltpu.make_async_copy(a, b, lsem.at[n])
+
+    def cache_copies(t):
+        b = lax.rem(t, NBUF)
+        blk = pl.ds(t * STEP, STEP)
+        return (pltpu.make_async_copy(kc_ref.at[:, :, blk], kbuf.at[b], csem.at[0, b]),
+                pltpu.make_async_copy(vc_ref.at[:, :, blk], vbuf.at[b], csem.at[1, b]))
+
+    @pl.when(i == 0)
+    def _():
+        for t in range(NBUF - 1):
+            for cp in cache_copies(t):
+                cp.start()
+
+    @pl.when(i < NSTEP - NBUF + 1)
+    def _():
+        for cp in cache_copies(i + NBUF - 1):
+            cp.start()
 
     @pl.when(i == 0)
     def _():
@@ -160,7 +218,7 @@
             pl.semaphore_signal(sem, inc=1, device_id=dev, device_id_type=MESH)
         col = lax.broadcasted_iota(jnp.int32, (48, 512), 1)
         row = lax.broadcasted_iota(jnp.int32, (48, 512), 0)
-        jj = jnp.where(row >= G, row - G, row)
+        jj = (row >> 3) * 4 + (row & 3)
         head = (jj >= 6).astype(jnp.int32) + (jj >= 12).astype(jnp.int32) + (jj >= 18).astype(jnp.int32)
         pos[...] = jnp.where((col & 3) == head, col >> 2, 1 << 20)
         pl.semaphore_wait(sem, 3)
@@ -171,15 +229,18 @@
             local_copy(n).start()
 
     lane = lax.broadcasted_iota(jnp.int32, (48, D), 1)
-    low = lax.broadcasted_iota(jnp.int32, (48, D), 0) < G
-    low1 = lax.broadcasted_iota(jnp.int32, (48, 1), 0) < G
+    low = (lax.broadcasted_iota(jnp.int32, (48, D), 0) & 7) < 4
+    low1 = (lax.broadcasted_iota(jnp.int32, (48, 1), 0) & 7) < 4
 
     @pl.when(i < NSTEP)
     def _():
+        for cp in cache_copies(i):
+            cp.wait()
+        k_ref = kbuf.at[lax.rem(i, NBUF)]
         for xo in range(2):
             for co in range(2):
                 for pp in range(STEP // 2):
-                    q48 = q_ref[xo, co, pp * 48:(pp + 1) * 48, :]
+                    q48 = q_ref[:, xo, co, pp * 8:(pp + 1) * 8, :].reshape(48, D)
                     qbd = jnp.concatenate([jnp.where(low, q48, 0.0), jnp.where(low, 0.0, q48)], axis=1).astype(BF16)
                     kk = jnp.concatenate([k_ref[xo, co, 2 * pp], k_ref[xo, co, 2 * pp + 1]], axis=1)
                     sc = lax.dot_general(qbd, kk, (((1,), (1,)), ((), ())), preferred_element_type=F32)
@@ -189,6 +250,7 @@
 
     @pl.when(i < NSTEP)
     def _():
+        v_ref = vbuf.at[lax.rem(i, NBUF)]
         ch = i // SPC
         within = lax.rem(i, SPC)
         for xo in range(2):
@@ -202,8 +264,7 @@
                     vv = jnp.concatenate([v_ref[xo, co, 2 * pp], v_ref[xo, co, 2 * pp + 1]], axis=1)
                     o = jnp.dot(w.astype(BF16), vv, preferred_element_type=F32)
                     at = pl.multiple_of((i * STEP + 2 * pp) * G, 2 * G)
-                    acc[co, xo, pl.ds(at, G), :] = o[:G, :D]
-                    acc[co, xo, pl.ds(at + G, G), :] = o[G:, D:]
+                    acc[co, xo, pl.ds(at, 2 * G), :] = jnp.where(low, o[:, :D], o[:, D:])
                     idx = within * (STEP // 2) + pp
                     stats = jnp.where(lane == idx, m, jnp.where(lane == idx + NP, l, stats))
                 st[ch, co, xo] = stats
@@ -261,7 +322,9 @@
         krows = pl.ds(pl.multiple_of((ch * CR + 2 * n) * KV, 2 * KV), 2 * KV)
         rr = lax.broadcasted_iota(jnp.int32, (48, 8), 0)
         cc = lax.broadcasted_iota(jnp.int32, (48, 8), 1)
-        hot = ((rr >= cc * 6) & (rr < cc * 6 + 6)).astype(F32)
+        first = ((cc & 3) * 6)
+        jj = (rr >> 3) * 4 + (rr & 3)
+        hot = ((jj >= first) & (jj < first + 6) & (((rr >> 2) & 1) == (cc >> 2))).astype(F32)
         return jnp.dot(hot, ref[krows, :], preferred_element_type=F32)
 
     def ev_x(ch):
@@ -298,7 +361,8 @@
             vnf[...] = vnb[...].astype(F32)
 
         def body(n, rows, out):
-            val = jnp.sum(qown[rows, :].astype(BF16).astype(F32) * spread(knf, ch, n), axis=1, keepdims=True)
+            qq = qown[:, pl.ds(pl.multiple_of((ch * CR + 2 * n) * 4, 8), 8), :].reshape(48, D)
+            val = jnp.sum(qq.astype(BF16).astype(F32) * spread(knf, ch, n), axis=1, keepdims=True)
             return jnp.where(lane == n, val, out)
         sms[ch] = pairs(ch, body, jnp.zeros((48, D), F32)) * SCALE2
 
@@ -314,27 +378,35 @@
 
         def body(n, rows, carry):
             ctx = acc[c, x, rows, :] * pick(fa, n) + xrecv[rows, :] * pick(fb, n) + pick(fs, n) * spread(vnf, ch, n)
-            ctxf[ch, c, pl.ds(pl.multiple_of(n * 48, 48), 48), :] = ctx
+            for k in range(3):
+                lo, hi = ctx[16 * k:16 * k + 8], ctx[16 * k + 8:16 * k + 16]
+                at = pl.multiple_of(n * 48 + 8 * k, 8)
+                ctxf[ch, c, pl.ds(at, 8), :] = jnp.where(low[:8], lo, pltpu.roll(hi, 4, 0))
+                ctxf[ch, c, pl.ds(at + G, 8), :] = jnp.where(low[:8], pltpu.roll(lo, 4, 0), hi)
             return carry
         pairs(ch, body, 0)
         ctx_copy(ch).start()
 
-    def ev_proj(ch):
-        ctx_in(ch).wait_recv()
-        for j in range(G):
-            for half in range(2):
-                lhs[half * CR:(half + 1) * CR, j * D:(j + 1) * D] = ctxf[ch, half, pl.ds(j, CR, G), :].astype(BF16)
+    def ev_proj(group):
+        m = len(group)
+        for g, ch in enumerate(group):
+            ctx_in(ch).wait_recv()
+            for j in range(G):
+                for half in range(2):
+                    lhs[pl.ds((2 * g + half) * CR, CR), j * D:(j + 1) * D] = ctxf[ch, half, pl.ds(j, CR, G), :].astype(BF16)
+            if ch >= 4:
+                y_part(ch - 4).wait_send()
 
         def mm(n, _):
             cols = pl.ds(pl.multiple_of(n * 512, 512), 512)
-            part = jnp.dot(lhs[...], wo[:, cols], preferred_element_type=F32)
-            pout[ch % 4, 0, :, cols] = part[:CR]
-            pout[ch % 4, 1, :, cols] = part[CR:]
+            part = jnp.dot(lhs[:m * 2 * CR], wo[:, cols], preferred_element_type=F32)
+            for g, ch in enumerate(group):
+                for half in range(2):
+                    pout[ch % 4, half, :, cols] = part[(2 * g + half) * CR:(2 * g + half + 1) * CR]
             return 0
-        if ch >= 4:
-            y_part(ch - 4).wait_send()
         lax.fori_loop(0, HALF // 512, mm, 0)
-        y_part(ch).start()
+        for ch in group:
+            y_part(ch).start()
 
     def ev_sum(ch):
         y_part(ch).wait_recv()
@@ -349,11 +421,19 @@
         gather(KFY, ch, dev_y, c, own).start()
         gather(KFC, ch, dev_c, c, own).start()
 
+    def forward(ch):
+        if ch in XFWD:
+            return gather(KGY, ch, dev_x, c, own_y)
+        return gather(KGY, ch, dev_y, c, own_x)
+
     def ev_fwd(ch):
         gather(KFX, ch, dev_x, c, own_x).wait_recv()
-        gather(KGY, ch, dev_y, c, own_x).start()
+        if ch not in XFWD:
+            forward(ch).start()
         gather(KGCX, ch, dev_c, c, own_x).start()
         gather(KFY, ch, dev_y, c, own_y).wait_recv()
+        if ch in XFWD:
+            forward(ch).start()
         gather(KGCY, ch, dev_c, c, own_y).start()
 
     def ev_last(ch):
@@ -388,9 +468,10 @@
         ctx_copy(ch).wait_send()
         if ch >= NCH - 4:
             y_part(ch).wait_send()
-        for kind, dev, owner in ((KFX, dev_x, own), (KFY, dev_y, own), (KFC, dev_c, own), (KGY, dev_y, own_x),
+        for kind, dev, owner in ((KFX, dev_x, own), (KFY, dev_y, own), (KFC, dev_c, own),
                                  (KGCX, dev_c, own_x), (KGCY, dev_c, own_y), (KGCD, dev_c, own_xy)):
             gather(kind, ch, dev, c, owner).wait_send()
+        forward(ch).wait_send()
         if ch >= NCH - 2:
             out_copy(ch).wait()
 
@@ -403,38 +484,37 @@
 
 
 def schedule():
-    offs = (("core", 0), ("x", 1), ("self", 2), ("ctx", 6), ("proj", 7), ("sum", 10), ("fwd", 14), ("last", 17), ("out", 19))
-    order = {name: n for n, (name, _) in enumerate(offs)}
-    plan = {}
+    order = {name: n for n, name in enumerate(OFFS)}
+    plan = []
     for ch in range(NCH):
         first = SPC * (ch + 1) - 1
-        for name, off in offs:
-            plan.setdefault(min(first + off, NSTEP - 1 + 64), []).append((first + off, order[name], name, ch))
+        for name, off in OFFS.items():
+            if name != "proj":
+                plan.append((first + off, order[name], name, ch))
+    for group in GROUPS:
+        plan.append((SPC * (group[-1] + 1) - 1 + OFFS["proj"], order["proj"], "proj", group))
+    plan.sort()
     steps = {}
-    for at in sorted(plan):
-        for t, o, name, ch in sorted(plan[at]):
-            steps.setdefault(min(at, NSTEP), []).append((t, o, name, ch))
-    out = []
-    for at in sorted(steps):
-        out.append((at, tuple((name, ch) for _, _, name, ch in sorted(steps[at]))))
-    last = out[-1]
-    out[-1] = (last[0], last[1] + tuple(("drain", ch) for ch in range(NCH)))
-    return tuple(out)
+    for at, _, name, arg in plan:
+        steps.setdefault(min(int(at), NSTEP), []).append((name, arg))
+    steps[NSTEP] += [("drain", ch) for ch in range(NCH)]
+    return tuple((at, tuple(steps[at])) for at in sorted(steps))
 
 
 def attend(lengths, q, k_cache, v_cache, kn, vn, hidden, w_o):
     hbm = pl.BlockSpec(memory_space=pl.ANY)
     hold = NSTEP - 1
-    cache_spec = pl.BlockSpec((2, 2, STEP, 512, D), lambda i: (0, 0, jnp.minimum(i, hold), 0, 0))
     return pl.pallas_call(
         functools.partial(attn_kernel, schedule()),
         grid=(NSTEP + 1,),
         out_shape=jax.ShapeDtypeStruct((4, OWN, DM), BF16),
         in_specs=[pl.BlockSpec(memory_space=pltpu.SMEM),
-                  pl.BlockSpec((2, 2, STEP * G, D), lambda i: (0, 0, jnp.minimum(i, hold), 0)),
-                  cache_spec, cache_spec, hbm, hbm, hbm, hbm, hbm],
+                  pl.BlockSpec((6, 2, 2, STEP * 4, D), lambda i: (0, 0, 0, jnp.minimum(i, hold), 0)),
+                  hbm, hbm, hbm, hbm, hbm, hbm, hbm],
         out_specs=hbm,
         scratch_shapes=[
+            pltpu.VMEM((NBUF, 2, 2, STEP, 512, D), BF16),
+            pltpu.VMEM((NBUF, 2, 2, STEP, 512, D), BF16),
             pltpu.VMEM((48, 512), jnp.int32),
             pltpu.VMEM((2, 2, OWN * G, D), F32),
             pltpu.VMEM((NCH, 2, 2, 48, D), F32),
@@ -448,17 +528,18 @@
             pltpu.VMEM((NCH, CR, HALF), F32),
             pltpu.VMEM((2, 4, OWN, HALF), F32),
             pltpu.VMEM((G * D, HALF), BF16),
-            pltpu.VMEM((OWN * G, D), F32),
+            pltpu.VMEM((6, OWN * 4, D), F32),
             pltpu.VMEM((OWN * KV, D), BF16),
             pltpu.VMEM((OWN * KV, D), BF16),
             pltpu.VMEM((OWN * KV, D), F32),
             pltpu.VMEM((OWN * KV, D), F32),
             pltpu.VMEM((OWN, HALF), BF16),
             pltpu.VMEM((NCH, 2, CR * G, D), F32),
-            pltpu.VMEM((2 * CR, G * D), BF16),
+            pltpu.VMEM((4 * CR, G * D), BF16),
             pltpu.VMEM((2, 4, CR, DM), BF16),
             pltpu.VMEM((2 * STEP, 48, 512), F32),
             pltpu.VMEM((NCH, 48, D), F32),
+            pltpu.SemaphoreType.DMA((2, NBUF)),
             pltpu.SemaphoreType.DMA((5,)),
             pltpu.SemaphoreType.DMA((2,)),
             pltpu.SemaphoreType.DMA((NKIND, NCH)),
@@ -481,8 +562,9 @@
         cos_t = jnp.concatenate([cos, cos, jnp.ones((ROWS, 2 * half), F32)], axis=1)
         s1_t = jnp.concatenate([-sin, zero, zero, zero], axis=1)
         s2_t = jnp.concatenate([zero, sin, zero, zero], axis=1)
-        q, kn, vn = project(hidden, ln_gain.reshape(1, DM), ln_bias.reshape(1, DM), cos_t, s1_t, s2_t, w_q, w_k, w_v)
-        out = attend(lengths, q.reshape(2, 2, OWN * G, D),
+        gb = jnp.stack([1.0 + ln_gain.astype(F32), ln_bias.astype(F32)])
+        q, kn, vn = project(hidden, gb, cos_t, s1_t, s2_t, w_q, w_k, w_v)
+        out = attend(lengths, q.reshape(6, 2, 2, OWN * 4, D),
                      k_cache.reshape(2, 2, OWN, 512, D), v_cache.reshape(2, 2, OWN, 512, D),
                      kn.reshape(2, 2, OWN * KV, D), vn.reshape(2, 2, OWN * KV, D),
                      hidden.reshape(2, 2, OWN, DM), w_o)

time: 178 us -> 145 us (0.81)
  Pallas kernels: 167 us -> 132 us
  other arithmetic: 1.89 us -> 4.73 us
    pallas_call x1, Pallas kernels: 38.8 us -> 20.8 us  [project(): pl.pallas_call(qkv_kernel, grid=(5,), out_shape=(jax.ShapeDtypeStruct((6,...]
    pallas_call x1, Pallas kernels: 128 us -> 111 us  [attend(): pl.pallas_call(functools.partial(attn_kernel, schedule()), grid=(NSTEP +...]
    unnamed x3 -> x7, local copies, waits for them, and re-layouts: 6.88 us -> 6.38 us
where the time goes in v3:
time: 145 us
  Pallas kernels  132 us (91%)
  local copies, waits for them, and re-layouts  7.26 us (5%)
  other arithmetic  4.73 us (3%)
    pallas_call x1, Pallas kernels, attend(): pl.pallas_call(functools.partial(attn_kernel, schedule()), grid=(NSTEP +...  111 us
    pallas_call x1, Pallas kernels, project(): pl.pallas_call(qkv_kernel, grid=(5,), out_shape=(jax.ShapeDtypeStruct((6,...  20.8 us
    unnamed x7, local copies, waits for them, and re-layouts  6.38 us

profile of v3, /device:TPU:0, one launch (start us, length us, event | category | flops | bytes accessed | tf_op | source)
XLA Modules:
  0.0 144.6 jit_solution(4501566601892991355)
XLA Ops:
  0.6 0.1 pad.6.clone
  0.7 0.1 pad.3.clone
  0.8 0.7 convert_element_type.8
  1.5 0.7 convert_add_fusion
  2.2 0.7 stack.16
  2.9 0.6 pad_maximum_fusion.gb_ref
  3.5 1.0 multiply_sine_fusion
  4.5 1.0 maximum_maximum_fusion
  5.5 0.7 concatenate.14.s1_ref
  6.3 20.8 %qkv.1 = (f32[6,2048,128]{2,1,0:T(8,128)}, bf16[2048,128]{1,0:T(8,128)(2,1)}, bf16[2048,128]{1,0:T(8,128)(2,1)}) custom-call(bf16[512,4096]{1,0:T(8,128)(2,1)} %h_ref.1, f32[2,4096]{1,0:T(2,128)} %pad_maximum_fusion.gb_ref, f32[512,128]{1,0:T(8,128)} %get-tuple-element.12.cos_ref, f32[512,128]{1,0:T(8,128)} %concatenate.14.s1_ref, ...), custom_call_target="tpu_custom_call" | custom-call | flops 8589934592 | bytes 33554432 | tf_op jit(solution)/shard_map/qkv/pallas_call | solution.py:149
  27.1 111.1 %attend.1 = bf16[4,128,4096]{2,1,0:T(8,128)(2,1)} custom-call(s32[512]{0:T(512)} %lens_ref.1, f32[6,2,2,512,128]{4,3,2,1,0:T(8,128)} %bitcast.11, bf16[2,2,128,512,128]{4,3,2,1,0:T(8,128)(2,1)} %bitcast.3.kc_ref, bf16[2,2,128,512,128]{4,3,2,1,0:T(8,128)(2,1)} %bitcast.4.vc_ref, f32[6,2,2,512,128]{4,3,2,1,0:T(8,128)} %bitcast.12, ...), custom_call_target="tpu_custom_call" | custom-call | flops 10000000000 | bytes 178257920 | tf_op jit(solution)/shard_map/attend/pallas_call | solution.py:507
  138.2 0.0 copy-start.1
  138.2 0.0 copy-start
  138.2 4.8 %copy.16 = bf16[512,4096]{1,0:T(8,128)(2,1)} copy(bf16[512,4096]{1,0:T(8,128)(2,1)} %bitcast.13) | data formatting | bytes 8388608
  143.0 0.0 copy-done.1
  143.0 0.8 copy.17
  143.8 0.0 copy-done
  143.8 0.8 copy.18
  (5 shorter events, 0.0 us)
Async XLA Ops:
  138.2 4.8 %copy-start.1 = (bf16[2048,128]{1,0:T(8,128)(2,1)S(1)}, bf16[2048,128]{1,0:T(8,128)(2,1)}, u32[]{:S(2)}) copy-start(bf16[2048,128]{1,0:T(8,128)(2,1)} %get-tuple-element.7) | copy-start | bytes 1572868
  138.2 5.6 %copy-start = (bf16[2048,128]{1,0:T(8,128)(2,1)S(1)}, bf16[2048,128]{1,0:T(8,128)(2,1)}, u32[]{:S(2)}) copy-start(bf16[2048,128]{1,0:T(8,128)(2,1)} %get-tuple-element.8) | copy-start | bytes 1572868

commit v4 on v3

--- a/solution.py
+++ b/solution.py
@@ -311,15 +311,15 @@
 
     def pairs(ch, body, init):
         def four(t, carry):
-            for u in range(4):
-                n = t * 4 + u
-                rows = pl.ds(pl.multiple_of((ch * CR + 2 * n) * G, 2 * G), 2 * G)
+            for u in range(NP):
+                n = t * NP + u
+                rows = pl.ds((ch * CR + 2 * n) * G, 2 * G)
                 carry = body(n, rows, carry)
             return carry
-        return lax.fori_loop(0, CR // 8, four, init)
+        return four(0, init)
 
     def spread(ref, ch, n):
-        krows = pl.ds(pl.multiple_of((ch * CR + 2 * n) * KV, 2 * KV), 2 * KV)
+        krows = pl.ds((ch * CR + 2 * n) * KV, 2 * KV)
         rr = lax.broadcasted_iota(jnp.int32, (48, 8), 0)
         cc = lax.broadcasted_iota(jnp.int32, (48, 8), 1)
         first = ((cc & 3) * 6)
@@ -361,7 +361,7 @@
             vnf[...] = vnb[...].astype(F32)
 
         def body(n, rows, out):
-            qq = qown[:, pl.ds(pl.multiple_of((ch * CR + 2 * n) * 4, 8), 8), :].reshape(48, D)
+            qq = qown[:, pl.ds((ch * CR + 2 * n) * 4, 8), :].reshape(48, D)
             val = jnp.sum(qq.astype(BF16).astype(F32) * spread(knf, ch, n), axis=1, keepdims=True)
             return jnp.where(lane == n, val, out)
         sms[ch] = pairs(ch, body, jnp.zeros((48, D), F32)) * SCALE2
@@ -380,7 +380,7 @@
             ctx = acc[c, x, rows, :] * pick(fa, n) + xrecv[rows, :] * pick(fb, n) + pick(fs, n) * spread(vnf, ch, n)
             for k in range(3):
                 lo, hi = ctx[16 * k:16 * k + 8], ctx[16 * k + 8:16 * k + 16]
-                at = pl.multiple_of(n * 48 + 8 * k, 8)
+                at = n * 48 + 8 * k
                 ctxf[ch, c, pl.ds(at, 8), :] = jnp.where(low[:8], lo, pltpu.roll(hi, 4, 0))
                 ctxf[ch, c, pl.ds(at + G, 8), :] = jnp.where(low[:8], pltpu.roll(lo, 4, 0), hi)
             return carry

time: 145 us -> 142 us (0.979)
  Pallas kernels: 132 us -> 129 us
    pallas_call x1, Pallas kernels: 111 us -> 108 us  [attend(): pl.pallas_call(functools.partial(attn_kernel, schedule()), grid=(NSTEP +...]
where the time goes in v4:
time: 142 us
  Pallas kernels  129 us (91%)
  local copies, waits for them, and re-layouts  7.26 us (5%)
  other arithmetic  4.73 us (3%)
    pallas_call x1, Pallas kernels, attend(): pl.pallas_call(functools.partial(attn_kernel, schedule()), grid=(NSTEP +...  108 us
    pallas_call x1, Pallas kernels, project(): pl.pallas_call(qkv_kernel, grid=(5,), out_shape=(jax.ShapeDtypeStruct((6,...  20.8 us
    unnamed x7, local copies, waits for them, and re-layouts  6.38 us

profile of v4, /device:TPU:0, one launch (start us, length us, event | category | flops | bytes accessed | tf_op | source)
XLA Modules:
  0.0 142.0 jit_solution(1483211981071642938)
XLA Ops:
  0.6 0.1 pad.6.clone
  0.7 0.1 pad.3.clone
  0.8 0.7 convert_element_type.8
  1.5 0.7 convert_add_fusion
  2.2 0.7 stack.16
  2.9 0.6 pad_maximum_fusion.gb_ref
  3.5 1.0 multiply_sine_fusion
  4.5 1.0 maximum_maximum_fusion
  5.5 0.7 concatenate.14.s1_ref
  6.3 20.8 %qkv.1 = (f32[6,2048,128]{2,1,0:T(8,128)}, bf16[2048,128]{1,0:T(8,128)(2,1)}, bf16[2048,128]{1,0:T(8,128)(2,1)}) custom-call(bf16[512,4096]{1,0:T(8,128)(2,1)} %h_ref.1, f32[2,4096]{1,0:T(2,128)} %pad_maximum_fusion.gb_ref, f32[512,128]{1,0:T(8,128)} %get-tuple-element.12.cos_ref, f32[512,128]{1,0:T(8,128)} %concatenate.14.s1_ref, ...), custom_call_target="tpu_custom_call" | custom-call | flops 8589934592 | bytes 33554432 | tf_op jit(solution)/shard_map/qkv/pallas_call | solution.py:149
  27.1 108.5 %attend.1 = bf16[4,128,4096]{2,1,0:T(8,128)(2,1)} custom-call(s32[512]{0:T(512)} %lens_ref.1, f32[6,2,2,512,128]{4,3,2,1,0:T(8,128)} %bitcast.11, bf16[2,2,128,512,128]{4,3,2,1,0:T(8,128)(2,1)} %bitcast.3.kc_ref, bf16[2,2,128,512,128]{4,3,2,1,0:T(8,128)(2,1)} %bitcast.4.vc_ref, f32[6,2,2,512,128]{4,3,2,1,0:T(8,128)} %bitcast.12, ...), custom_call_target="tpu_custom_call" | custom-call | flops 10000000000 | bytes 178257920 | tf_op jit(solution)/shard_map/attend/pallas_call | solution.py:507
  135.6 0.0 copy-start.1
  135.6 0.0 copy-start
  135.6 4.8 %copy.16 = bf16[512,4096]{1,0:T(8,128)(2,1)} copy(bf16[512,4096]{1,0:T(8,128)(2,1)} %bitcast.13) | data formatting | bytes 8388608
  140.4 0.0 copy-done.1
  140.4 0.8 copy.17
  141.2 0.0 copy-done
  141.2 0.8 copy.18
  (5 shorter events, 0.0 us)
Async XLA Ops:
  135.6 4.8 %copy-start.1 = (bf16[2048,128]{1,0:T(8,128)(2,1)S(1)}, bf16[2048,128]{1,0:T(8,128)(2,1)}, u32[]{:S(2)}) copy-start(bf16[2048,128]{1,0:T(8,128)(2,1)} %get-tuple-element.7) | copy-start | bytes 1572868
  135.6 5.6 %copy-start = (bf16[2048,128]{1,0:T(8,128)(2,1)S(1)}, bf16[2048,128]{1,0:T(8,128)(2,1)}, u32[]{:S(2)}) copy-start(bf16[2048,128]{1,0:T(8,128)(2,1)} %get-tuple-element.8) | copy-start | bytes 1572868
